TPU v7x, 32 devices: a whole 2x2x4 slice. The times are simulated.
32 devices in a mesh: cp: 8 (over z, core), fsdp: 4 (over y, x).
Axes of the slice: x: 2, y: 2, z: 4, core: 2. Of those that a mesh axis runs over, the one named last changes fastest.
Arguments:
- tokens: bfloat16 [4, 16, 64, 2304], P('fsdp', 'cp'), may hold values from -6 to 6
- gains: float32 [4, 2304], replicated, may hold values from 0.25 to 1.75
- w_query: bfloat16 [2304, 2048], P(('cp', 'fsdp')), may hold values from -0.125 to 0.125
- w_key: bfloat16 [2304, 1024], P(('cp', 'fsdp')), may hold values from -0.125 to 0.125
- w_value: bfloat16 [2304, 1024], P(('cp', 'fsdp')), may hold values from -0.125 to 0.125
- w_out: bfloat16 [2304, 2048], P(('cp', 'fsdp')), may hold values from -0.125 to 0.125
- w_gate: bfloat16 [2304, 9216], P(('cp', 'fsdp')), may hold values from -0.125 to 0.125
- w_up: bfloat16 [2304, 9216], P(('cp', 'fsdp')), may hold values from -0.125 to 0.125
- w_down: bfloat16 [2304, 9216], P(('cp', 'fsdp')), may hold values from -0.0625 to 0.0625
- order: int32 [16], replicated, may hold values from 0 to 15, as said below
- cotangent: bfloat16 [4, 16, 64, 2304], P('fsdp', 'cp'), may hold values from -6 to 6
Outputs:
- output: bfloat16 [4, 16, 64, 2304], P('fsdp', 'cp')
- grad_tokens: float32 [4, 16, 64, 2304], P('fsdp', 'cp')
- grad_gains: float32 [4, 2304], P(None, ('cp', 'fsdp'))
- grad_query: float32 [2304, 2048], P(('cp', 'fsdp'))
- grad_key: float32 [2304, 1024], P(('cp', 'fsdp'))
- grad_value: float32 [2304, 1024], P(('cp', 'fsdp'))
- grad_out: float32 [2304, 2048], P(('cp', 'fsdp'))
- grad_gate: float32 [2304, 9216], P(('cp', 'fsdp'))
- grad_up: float32 [2304, 9216], P(('cp', 'fsdp'))
- grad_down: float32 [2304, 9216], P(('cp', 'fsdp'))
Inputs may be any that keep to these rules, and one draw needn't show every extreme that they name: order is a permutation of the causal block numbers; stored blocks 2c and 2c + 1 hold two blocks whose numbers add up to 15, in either order.
All inputs are finite; a program needn't handle non-finite values.
Results may differ from a plain program's by a relative error of at most 0.022.
Values may be sent and summed in bfloat16 or wider, within the bound.
A program may use at most 320 MiB of HBM per device.

v0:
```python
from functools import partial
import math

import jax
import jax.numpy as jnp
from jax import lax
from jax.sharding import PartitionSpec as P

HEADS = 8
KV_HEADS = 4
HEAD = 256


SOFT_CAP = 50.0
NORM_EPS = 1e-06
ROPE_BASE = 10000.0
CONTRACT_LAST = (((1,), (1,)), ((), ()))
CONTRACT_FIRST = (((0,), (0,)), ((), ()))


def normalize(values):
    factor = lax.rsqrt(jnp.mean(values * values, axis=-1, keepdims=True) + NORM_EPS)
    return (values * factor, factor)


def norm_back(grad_normed, normed, factor):
    return factor * (grad_normed - normed * jnp.mean(grad_normed * normed, axis=-1, keepdims=True))


def rotary(values, cosine, sine, direction):
    middle = values.shape[-1] // 2
    first = values[..., :middle]
    second = values[..., middle:]
    cos_b = cosine[:, None, :]
    sin_b = sine[:, None, :] * direction
    return jnp.concatenate(
        [first * cos_b - second * sin_b, second * cos_b + first * sin_b], axis=-1
    )


def local(tokens, gains, w_query, w_key, w_value, w_out, w_gate, w_up, w_down, order, cotangent):
    width = tokens.shape[-1]
    span = tokens.shape[2]
    q_width = w_query.shape[1]
    kv_width = w_key.shape[1]
    groups = HEADS // KV_HEADS
    scale_q = HEAD ** (-0.5)
    context = lax.axis_index("cp")
    local_order = lax.dynamic_slice_in_dim(order, 2 * context, 2)
    offsets = jnp.arange(span, dtype=jnp.int32)
    local_pos = (local_order[:, None] * span + offsets[None, :]).reshape(-1)
    every_pos = (order[:, None] * span + offsets[None, :]).reshape(-1)
    visible = every_pos[None, :] <= local_pos[:, None]
    inverse = jnp.exp(-math.log(ROPE_BASE) * jnp.arange(HEAD // 2, dtype=jnp.float32) * 2.0 / HEAD)
    angle = local_pos.astype(jnp.float32)[:, None] * inverse[None, :]
    cosine = jnp.cos(angle)
    sine = jnp.sin(angle)
    hidden = tokens.reshape(-1, width).astype(jnp.float32)
    count_rows = hidden.shape[0]
    normed_one, factor_one = normalize(hidden)
    attn_in = (normed_one * gains[0]).astype(jnp.bfloat16)
    pieces = (
        lax.all_gather(w_query, ("cp", "fsdp"), axis=0, tiled=True),
        lax.all_gather(w_key, ("cp", "fsdp"), axis=0, tiled=True),
        lax.all_gather(w_value, ("cp", "fsdp"), axis=0, tiled=True),
    )
    columns = attn_in
    q_lin, k_lin, v_lin = tuple(
        (jnp.dot(columns, piece, preferred_element_type=jnp.float32) for piece in pieces)
    )
    query_low = rotary(q_lin.reshape(count_rows, HEADS, HEAD), cosine, sine, 1.0).astype(
        jnp.bfloat16
    )
    key_low = rotary(k_lin.reshape(count_rows, KV_HEADS, HEAD), cosine, sine, 1.0).astype(
        jnp.bfloat16
    )
    value_low = v_lin.astype(jnp.bfloat16)
    query_groups = query_low.reshape(count_rows, KV_HEADS, groups, HEAD)

    def share_keys():
        blocks = (
            lax.all_gather(key_low.reshape(2, span, kv_width), "cp", axis=0, tiled=True),
            lax.all_gather(value_low.reshape(2, span, kv_width), "cp", axis=0, tiled=True),
        )
        return (blocks[0].reshape(-1, KV_HEADS, HEAD), blocks[1].reshape(-1, KV_HEADS, HEAD))

    def bent_scores(keys_all):
        raw = (
            jnp.einsum("tkgd,skd->kgts", query_groups, keys_all, preferred_element_type=jnp.float32)
            * scale_q
        )
        return jnp.tanh(raw / SOFT_CAP)

    keys_all, values_all = share_keys()
    bent = bent_scores(keys_all)
    scores = jnp.where(visible, SOFT_CAP * bent, -1e30)
    top_score = jnp.max(scores, axis=-1, keepdims=True)
    expo = jnp.exp(scores - top_score)
    total_mass = jnp.sum(expo, axis=-1, keepdims=True)
    log_total = top_score + jnp.log(total_mass)
    probs_low = (expo / total_mass).astype(jnp.bfloat16)
    attended = jnp.einsum(
        "kgts,skd->tkgd", probs_low, values_all, preferred_element_type=jnp.float32
    )
    attended_low = attended.reshape(count_rows, q_width).astype(jnp.bfloat16)
    attn_out = lax.dot_general(
        attended_low,
        lax.all_gather(w_out, ("cp", "fsdp"), axis=0, tiled=True),
        CONTRACT_LAST,
        preferred_element_type=jnp.float32,
    )
    normed_two, factor_two = normalize(attn_out)
    middle_sum = hidden + normed_two * gains[1]
    normed_three, factor_three = normalize(middle_sum)
    ffn_in = (normed_three * gains[2]).astype(jnp.bfloat16)
    relayed = (
        lax.all_to_all(w_gate, "fsdp", split_axis=1, concat_axis=0, tiled=True),
        lax.all_to_all(w_up, "fsdp", split_axis=1, concat_axis=0, tiled=True),
        lax.all_to_all(w_down, "fsdp", split_axis=1, concat_axis=0, tiled=True),
    )
    gate_part, up_part, down_part = (
        lax.all_gather(relayed[0], "cp", axis=0, tiled=True),
        lax.all_gather(relayed[1], "cp", axis=0, tiled=True),
        lax.all_gather(relayed[2], "cp", axis=0, tiled=True),
    )
    group_in = lax.all_gather(ffn_in, "fsdp", axis=0, tiled=True)
    gate = jnp.dot(group_in, gate_part, preferred_element_type=jnp.float32)
    upper = jnp.dot(group_in, up_part, preferred_element_type=jnp.float32)
    activated = jax.nn.gelu(gate, approximate=True)
    inner_low = (activated * upper).astype(jnp.bfloat16)
    share_out = lax.dot_general(
        inner_low, down_part, CONTRACT_LAST, preferred_element_type=jnp.float32
    )
    ffn_out = lax.psum_scatter(
        share_out.astype(jnp.bfloat16), "fsdp", scatter_dimension=0, tiled=True
    ).astype(jnp.float32)
    normed_four, factor_four = normalize(ffn_out)
    result = middle_sum + normed_four * gains[3]
    output = result.astype(jnp.bfloat16).reshape(tokens.shape)
    grad_result = cotangent.reshape(-1, width).astype(jnp.float32)
    gain_four = jnp.sum(grad_result * normed_four, axis=0)
    grad_ffn_low = norm_back(grad_result * gains[3], normed_four, factor_four).astype(jnp.bfloat16)
    group_grad = lax.all_gather(grad_ffn_low, "fsdp", axis=0, tiled=True)
    grad_inner = jnp.dot(group_grad, down_part, preferred_element_type=jnp.float32)
    unused_value, gelu_back = jax.vjp(partial(jax.nn.gelu, approximate=True), gate)
    grad_gate_low = gelu_back(grad_inner * upper)[0].astype(jnp.bfloat16)
    grad_upper_low = (grad_inner * activated).astype(jnp.bfloat16)
    share_in = lax.dot_general(
        grad_gate_low, gate_part, CONTRACT_LAST, preferred_element_type=jnp.float32
    ) + lax.dot_general(grad_upper_low, up_part, CONTRACT_LAST, preferred_element_type=jnp.float32)
    grad_ffn_in = lax.psum_scatter(
        share_in.astype(jnp.bfloat16), "fsdp", scatter_dimension=0, tiled=True
    ).astype(jnp.float32)
    part_width = gate_part.shape[1]
    slice_sums = lax.psum_scatter(
        jnp.concatenate(
            [
                lax.dot_general(
                    group_in, grad_gate_low, CONTRACT_FIRST, preferred_element_type=jnp.float32
                ),
                lax.dot_general(
                    group_in, grad_upper_low, CONTRACT_FIRST, preferred_element_type=jnp.float32
                ),
                lax.dot_general(
                    group_grad, inner_low, CONTRACT_FIRST, preferred_element_type=jnp.float32
                ),
            ],
            axis=1,
        ).astype(jnp.bfloat16),
        "cp",
        scatter_dimension=0,
        tiled=True,
    ).astype(jnp.float32)
    grad_gate, grad_up, grad_down = (
        lax.all_to_all(
            slice_sums[:, :part_width].astype(jnp.bfloat16),
            "fsdp",
            split_axis=0,
            concat_axis=1,
            tiled=True,
        ).astype(jnp.float32),
        lax.all_to_all(
            slice_sums[:, part_width : 2 * part_width].astype(jnp.bfloat16),
            "fsdp",
            split_axis=0,
            concat_axis=1,
            tiled=True,
        ).astype(jnp.float32),
        lax.all_to_all(
            slice_sums[:, 2 * part_width :].astype(jnp.bfloat16),
            "fsdp",
            split_axis=0,
            concat_axis=1,
            tiled=True,
        ).astype(jnp.float32),
    )
    gain_three = jnp.sum(grad_ffn_in * normed_three, axis=0)
    grad_middle = grad_result + norm_back(grad_ffn_in * gains[2], normed_three, factor_three)
    gain_two = jnp.sum(grad_middle * normed_two, axis=0)
    grad_attn_low = norm_back(grad_middle * gains[1], normed_two, factor_two).astype(jnp.bfloat16)
    columns = grad_attn_low
    grad_attended = jnp.dot(
        columns,
        lax.all_gather(w_out, ("cp", "fsdp"), axis=0, tiled=True),
        preferred_element_type=jnp.float32,
    )
    grad_att_low = grad_attended.astype(jnp.bfloat16).reshape(count_rows, KV_HEADS, groups, HEAD)
    keys_back, values_back = share_keys()
    bent_back = bent_scores(keys_back)
    probs_full = jnp.where(visible, jnp.exp(SOFT_CAP * bent_back - log_total), 0.0)
    probs_back = probs_full.astype(jnp.bfloat16)
    grad_probs = jnp.einsum(
        "tkgd,skd->kgts", grad_att_low, values_back, preferred_element_type=jnp.float32
    )
    delta = jnp.sum(grad_probs * probs_full, axis=-1, keepdims=True)
    grad_raw = (probs_full * (grad_probs - delta) * (1.0 - bent_back * bent_back)).astype(
        jnp.bfloat16
    )
    grad_query_rot = (
        jnp.einsum("kgts,skd->tkgd", grad_raw, keys_back, preferred_element_type=jnp.float32)
        * scale_q
    )
    grad_keys_all = (
        jnp.einsum("kgts,tkgd->skd", grad_raw, query_groups, preferred_element_type=jnp.float32)
        * scale_q
    )
    grad_values_all = jnp.einsum(
        "kgts,tkgd->skd", probs_back, grad_att_low, preferred_element_type=jnp.float32
    )
    slots = order.shape[0]
    grad_keys, grad_values = (
        lax.psum_scatter(
            grad_keys_all.reshape(slots, span, kv_width).astype(jnp.bfloat16),
            "cp",
            scatter_dimension=0,
            tiled=True,
        ).astype(jnp.float32),
        lax.psum_scatter(
            grad_values_all.reshape(slots, span, kv_width).astype(jnp.bfloat16),
            "cp",
            scatter_dimension=0,
            tiled=True,
        ).astype(jnp.float32),
    )
    grad_q_low = (
        rotary(grad_query_rot.reshape(count_rows, HEADS, HEAD), cosine, sine, -1.0)
        .reshape(count_rows, q_width)
        .astype(jnp.bfloat16)
    )
    grad_k_low = (
        rotary(grad_keys.reshape(count_rows, KV_HEADS, HEAD), cosine, sine, -1.0)
        .reshape(count_rows, kv_width)
        .astype(jnp.bfloat16)
    )
    grad_v_low = grad_values.reshape(count_rows, kv_width).astype(jnp.bfloat16)
    pieces = lax.all_gather((w_query, w_key, w_value), ("cp", "fsdp"), axis=0, tiled=True)
    grad_attn_in = (
        lax.dot_general(grad_q_low, pieces[0], CONTRACT_LAST, preferred_element_type=jnp.float32)
        + lax.dot_general(grad_k_low, pieces[1], CONTRACT_LAST, preferred_element_type=jnp.float32)
        + lax.dot_general(grad_v_low, pieces[2], CONTRACT_LAST, preferred_element_type=jnp.float32)
    )
    gain_one = jnp.sum(grad_attn_in * normed_one, axis=0)
    grad_hidden = grad_middle + norm_back(grad_attn_in * gains[0], normed_one, factor_one)
    gain_columns = jnp.stack([gain_one, gain_two, gain_three, gain_four], axis=1)
    attn_terms = jnp.concatenate(
        [
            lax.dot_general(
                attn_in, grad_q_low, CONTRACT_FIRST, preferred_element_type=jnp.float32
            ),
            lax.dot_general(
                attn_in, grad_k_low, CONTRACT_FIRST, preferred_element_type=jnp.float32
            ),
            lax.dot_general(
                attn_in, grad_v_low, CONTRACT_FIRST, preferred_element_type=jnp.float32
            ),
            lax.dot_general(
                grad_attn_low, attended_low, CONTRACT_FIRST, preferred_element_type=jnp.float32
            ),
            gain_columns,
        ],
        axis=1,
    )
    attn_sums = lax.psum_scatter(attn_terms, ("cp", "fsdp"), scatter_dimension=0, tiled=True)
    grad_query = attn_sums[:, :q_width]
    grad_key = attn_sums[:, q_width : q_width + kv_width]
    grad_value = attn_sums[:, q_width + kv_width : q_width + 2 * kv_width]
    grad_out = attn_sums[:, q_width + 2 * kv_width : 2 * q_width + 2 * kv_width]
    grad_gains = attn_sums[:, 2 * q_width + 2 * kv_width :].T
    return (
        output,
        grad_hidden.reshape(tokens.shape),
        grad_gains,
        grad_query,
        grad_key,
        grad_value,
        grad_out,
        grad_gate,
        grad_up,
        grad_down,
    )


def solution(mesh):
    return jax.shard_map(
        local,
        mesh=mesh,
        in_specs=(
            P("fsdp", "cp", None, None),
            P(),
            P(("cp", "fsdp"), None),
            P(("cp", "fsdp"), None),
            P(("cp", "fsdp"), None),
            P(("cp", "fsdp"), None),
            P(("cp", "fsdp"), None),
            P(("cp", "fsdp"), None),
            P(("cp", "fsdp"), None),
            P(),
            P("fsdp", "cp", None, None),
        ),
        out_specs=(
            P("fsdp", "cp", None, None),
            P("fsdp", "cp", None, None),
            P(None, ("cp", "fsdp")),
            P(("cp", "fsdp"), None),
            P(("cp", "fsdp"), None),
            P(("cp", "fsdp"), None),
            P(("cp", "fsdp"), None),
            P(("cp", "fsdp"), None),
            P(("cp", "fsdp"), None),
            P(("cp", "fsdp"), None),
        ),
        check_vma=False,
    )
```

profile of v0, /device:TPU:9, one launch (start us, length us, event | category | flops | bytes accessed | tf_op | source)
XLA Modules:
  0.0 2170.8 jit_solution(5606503408207854462)
XLA Ops:
  14.8 61.1 %all-gather.16.cloned.1.call-done = bf16[2304,1024]{1,0:T(8,128)(2,1)} async-done(((bf16[72,1024]{1,0:T(8,128)(2,1)}), bf16[2304,1024]{1,0:T(8,128)(2,1)}) %all-gather.16.cloned.1.call-update) | async-done | bytes 4718608 | tf_op jit(solution)/shard_map/all_gather | solution.py:64
  75.9 6.8 copy.103
  88.3 52.3 %all-gather.12.cloned.1.call-done = bf16[2304,1024]{1,0:T(8,128)(2,1)} async-done(((bf16[72,1024]{1,0:T(8,128)(2,1)}), bf16[2304,1024]{1,0:T(8,128)(2,1)}) %all-gather.12.cloned.1.call-update) | async-done | bytes 4718608 | tf_op jit(solution)/shard_map/all_gather | solution.py:65
  145.8 20.4 all_to_all.96
  176.8 24.2 %all-gather.14.cloned.1.call-done = bf16[16,64,1024]{2,1,0:T(8,128)(2,1)} async-done(((bf16[2,64,1024]{2,1,0:T(8,128)(2,1)}), bf16[16,64,1024]{2,1,0:T(8,128)(2,1)}) %all-gather.14.cloned.1.call-update) | async-done | bytes 2097168 | tf_op jit(solution)/shard_map/all_gather | solution.py:83
  204.3 80.1 %all-gather.20.cloned.1.call-done = bf16[2304,2048]{1,0:T(8,128)(2,1)} async-done(((bf16[72,2048]{1,0:T(8,128)(2,1)}), bf16[2304,2048]{1,0:T(8,128)(2,1)}) %all-gather.20.cloned.1.call-update) | async-done | bytes 9437200 | tf_op jit(solution)/shard_map/all_gather | solution.py:63
  284.4 12.1 copy.105
  296.6 7.0 fusion.112
  309.2 58.0 %all-gather.22.cloned.1.call-done = bf16[2304,2048]{1,0:T(8,128)(2,1)} async-done(((bf16[72,2048]{1,0:T(8,128)(2,1)}), bf16[2304,2048]{1,0:T(8,128)(2,1)}) %all-gather.22.cloned.1.call-update) | async-done | bytes 9437200 | tf_op jit(solution)/shard_map/all_gather | solution.py:108
  367.2 7.0 multiply_reduce_fusion.3
  377.3 20.4 all_to_all.97
  399.2 19.5 all_to_all.98
  419.4 45.8 %all-gather.26.cloned.1.call-done = bf16[2304,2304]{1,0:T(8,128)(2,1)} async-done(((bf16[288,2304]{1,0:T(8,128)(2,1)}), bf16[2304,2304]{1,0:T(8,128)(2,1)}) %all-gather.26.cloned.1.call-update) | async-done | bytes 10616848 | tf_op jit(solution)/shard_map/all_gather | solution.py:122
  465.1 40.4 %all-gather.24.cloned.1.call-done = bf16[512,2304]{1,0:T(8,128)(2,1)} async-done(((bf16[128,2304]{1,0:T(8,128)(2,1)}), bf16[512,2304]{1,0:T(8,128)(2,1)}) %all-gather.24.cloned.1.call-update) | async-done | bytes 2359312 | tf_op jit(solution)/shard_map/all_gather | solution.py:126
  505.5 11.6 fusion.113
  517.1 88.3 %all-gather.28.cloned.1.call-done = bf16[2304,2304]{1,0:T(8,128)(2,1)} async-done(((bf16[288,2304]{1,0:T(8,128)(2,1)}), bf16[2304,2304]{1,0:T(8,128)(2,1)}) %all-gather.28.cloned.1.call-update) | async-done | bytes 10616848 | tf_op jit(solution)/shard_map/all_gather | solution.py:123
  605.4 12.8 multiply_convert_fusion.1
  618.2 87.5 %all-gather.30.cloned.1.call-done = bf16[2304,2304]{1,0:T(8,128)(2,1)} async-done(((bf16[288,2304]{1,0:T(8,128)(2,1)}), bf16[2304,2304]{1,0:T(8,128)(2,1)}) %all-gather.30.cloned.1.call-update) | async-done | bytes 10616848 | tf_op jit(solution)/shard_map/all_gather | solution.py:124
  705.7 11.4 convolution_convert_fusion.3
  717.1 38.0 %reduce-scatter.9.cloned.1.call-done = bf16[128,2304]{1,0:T(8,128)(2,1)} async-done(((bf16[512,2304]{1,0:T(8,128)(2,1)}), bf16[128,2304]{1,0:T(8,128)(2,1)}) %reduce-scatter.9.cloned.1.call-update) | async-done | bytes 589840 | tf_op jit(solution)/shard_map/reduce_scatter | solution.py:134
  761.1 37.3 %all-gather.32.cloned.1.call-done = bf16[512,2304]{1,0:T(8,128)(2,1)} async-done(((bf16[128,2304]{1,0:T(8,128)(2,1)}), bf16[512,2304]{1,0:T(8,128)(2,1)}) %all-gather.32.cloned.1.call-update) | async-done | bytes 2359312 | tf_op jit(solution)/shard_map/all_gather | solution.py:143
  798.4 14.2 multiply_convert_fusion
  812.6 9.8 fusion.114
  822.5 10.9 fusion.8
  835.0 36.0 %reduce-scatter.11.cloned.1.call-done = bf16[128,2304]{1,0:T(8,128)(2,1)} async-done(((bf16[512,2304]{1,0:T(8,128)(2,1)}), bf16[128,2304]{1,0:T(8,128)(2,1)}) %reduce-scatter.11.cloned.1.call-update) | async-done | bytes 589840 | tf_op jit(solution)/shard_map/reduce_scatter | solution.py:151
  878.6 5.3 convolution_convert_fusion.4
  886.9 11.1 fusion.46
  904.1 10.4 convolution_convert_fusion
  914.6 8.2 convolution_convert_fusion.1
  931.5 10.4 convolution_convert_fusion.2
  941.9 22.8 %pad_maximum_fusion = bf16[2304,6912]{0,1:T(8,128)(2,1)} fusion(bf16[2304,2304]{0,1:T(8,128)(2,1)} %convolution_convert_fusion, bf16[2304,2304]{0,1:T(8,128)(2,1)} %convolution_convert_fusion.1, bf16[2304,2304]{0,1:T(8,128)(2,1)} %convolution_convert_fusion.2), kind=kLoop, calls=%fused_computation.1 | loop fusion | flops 95551488 | bytes 63700992 | tf_op jit(solution)/shard_map/concatenate | solution.py:156
  964.7 38.3 %copy.158 = bf16[2304,6912]{1,0:T(8,128)(2,1)} copy(bf16[2304,6912]{0,1:T(8,128)(2,1)} %pad_maximum_fusion) | data formatting | bytes 63700992
  1005.5 9.8 fusion.57
  1016.3 7.1 fusion.115
  1023.5 8.0 fusion.119
  1031.4 8.1 fusion.117
  1041.9 4.2 convolution_add_fusion.2
  1046.2 4.9 fusion.80
  1051.1 5.0 fusion.116
  1056.1 4.9 fusion.118
  1061.1 129.5 %concatenate.32 = f32[2304,6148]{0,1:T(8,128)} concatenate(f32[2304,2048]{0,1:T(8,128)} %fusion.117, f32[2304,1024]{0,1:T(8,128)} %fusion.118, f32[2304,1024]{0,1:T(8,128)} %fusion.116, f32[2304,2048]{0,1:T(8,128)} %fusion.119, f32[2304,1]{0,1:T(1,128)S(1)} %stack.12, f32[2304,1]{0,1:T(1,128)S(1)} %copy-done.40, f32[2304,1]{0,1:T(1,128)S(1)} %copy-done.39, f32[2304,1]{0,1:T(1,128)S(1)} %copy-done.38), dimensions={1} | concatenate | bytes 113319936 | tf_op jit(solution)/shard_map/concatenate | solution.py:265
  1190.6 122.2 %reduce-scatter.17.cloned.1.call-done = bf16[288,6912]{1,0:T(8,128)(2,1)} async-done(((bf16[2304,6912]{1,0:T(8,128)(2,1)}), bf16[288,6912]{1,0:T(8,128)(2,1)}) %reduce-scatter.17.cloned.1.call-update) | async-done | bytes 3981328 | tf_op jit(solution)/shard_map/reduce_scatter | solution.py:155
  1312.8 4.1 fusion.109
  1316.9 4.4 all-to-all-start.5
  1321.4 28.7 %all-to-all-done.5 = bf16[4,72,2304]{2,1,0:T(8,128)(2,1)} async-done(((bf16[4,72,2304]{2,1,0:T(8,128)(2,1)}), bf16[4,72,2304]{2,1,0:T(8,128)(2,1)}, u32[]{:S(2)}, u32[]{:S(2)}) %all-to-all-start.5) | async-done | bytes 1327136 | tf_op jit(solution)/shard_map/all_to_all | solution.py:189
  1350.1 4.3 all-to-all-start.3
  1355.8 776.6 %all-reduce.3.cloned.1.call-done = f32[2304,6148]{0,1:T(8,128)} async-done(((f32[2304,6148]{0,1:T(8,128)}), f32[2304,6148]{0,1:T(8,128)}) %all-reduce.3.cloned.1.call-update) | async-done | bytes 56659984
  2152.6 9.6 all-to-all-done.4
  (231 shorter events, 104.8 us)
Async XLA Ops:
  7.2 68.7 %all-gather.16.cloned.1.call-start = ((), (), s32[]{:S(2)}) async-start(), calls=%async_computation.13 | async-start | bytes 4866048 | tf_op jit(solution)/shard_map/all_gather | solution.py:64
  7.9 132.7 %all-gather.12.cloned.1.call-start = ((), (), s32[]{:S(2)}) async-start(), calls=%async_computation.11 | async-start | bytes 4866048 | tf_op jit(solution)/shard_map/all_gather | solution.py:65
  8.7 161.7 %all-gather.18.cloned.1.call-start = ((), (), s32[]{:S(2)}) async-start(), calls=%async_computation.14 | async-start | bytes 2359296 | tf_op jit(solution)/shard_map/all_gather | solution.py:82
  11.3 76.8 %copy-start.27 = (f32[2304]{0:T(1024)}, f32[2304]{0:T(1024)S(1)}, u32[]{:S(2)}) copy-start(f32[2304]{0:T(1024)S(1)} %get-tuple-element.60) | copy-start | bytes 27652
  13.5 290.1 %copy-start.19 = (f32[128,128]{1,0:T(8,128)}, f32[128,128]{1,0:T(8,128)S(1)}, u32[]{:S(2)}) copy-start(f32[128,128]{1,0:T(8,128)S(1)} %get-tuple-element.87) | copy-start | bytes 196612
  14.8 281.8 %copy-start = (bf16[1,2,64,2304]{3,2,1,0:T(8,128)(2,1)}, bf16[1,2,64,2304]{3,2,1,0:T(8,128)(2,1)S(1)}, u32[]{:S(2)}) copy-start(bf16[1,2,64,2304]{3,2,1,0:T(8,128)(2,1)S(1)} %fusion.83) | copy-start | bytes 1769476
  87.0 58.7 %copy-start.21 = (bf16[72,9216]{1,0:T(8,128)(2,1)S(1)}, bf16[72,9216]{1,0:T(8,128)(2,1)}, u32[]{:S(2)}) copy-start(bf16[72,9216]{1,0:T(8,128)(2,1)} %param.17) | copy-start | bytes 3981316
  88.0 113.0 %all-gather.14.cloned.1.call-start = ((), (), s32[]{:S(2)}) async-start(), calls=%async_computation.12 | async-start | bytes 2359296 | tf_op jit(solution)/shard_map/all_gather | solution.py:83
  88.1 57.7 %copy-start.44 = (f32[128]{0:T(128)}, f32[128]{0:T(128)S(1)}, u32[]{:S(2)}) copy-start(f32[128]{0:T(128)S(1)} %rsqrt.37) | copy-start | bytes 1540
  144.5 22.1 %copy-start.51 = (s32[16]{0:T(128)S(1)}, s32[16]{0:T(128)}, u32[]{:S(2)}) copy-start(s32[16]{0:T(128)} %param.20) | copy-start | bytes 196
  144.5 140.0 %all-gather.20.cloned.1.call-start = ((), (), s32[]{:S(2)}) async-start(), calls=%async_computation.15 | async-start | bytes 9732096 | tf_op jit(solution)/shard_map/all_gather | solution.py:63
  145.1 222.1 %all-gather.22.cloned.1.call-start = ((), (), s32[]{:S(2)}) async-start(), calls=%async_computation.16 | async-start | bytes 9732096 | tf_op jit(solution)/shard_map/all_gather | solution.py:108
  145.6 319.5 %all-gather.26.cloned.1.call-start = ((), (), s32[]{:S(2)}) async-start(), calls=%async_computation.18 | async-start | bytes 11943936 | tf_op jit(solution)/shard_map/all_gather | solution.py:122
  166.2 339.3 %all-gather.24.cloned.1.call-start = ((), (), s32[]{:S(2)}) async-start(), calls=%async_computation.17 | async-start | bytes 2949120 | tf_op jit(solution)/shard_map/all_gather | solution.py:126
  166.9 139.5 %copy-start.25 = (pred[128,1024]{0,1:T(8,128)(4,1)}, pred[128,1024]{0,1:T(8,128)(4,1)S(1)}, u32[]{:S(2)}) copy-start(pred[128,1024]{0,1:T(8,128)(4,1)S(1)} %broadcast_compare_fusion) | copy-start | bytes 393220
  204.3 102.2 %copy-start.7 = (bf16[1024,4,256]{2,1,0:T(4,128)(2,1)}, bf16[1024,4,256]{2,1,0:T(4,128)(2,1)S(1)}, u32[]{:S(2)}) copy-start(bf16[1024,4,256]{2,1,0:T(4,128)(2,1)S(1)} %reshape.372) | copy-start | bytes 6291460
  296.6 7.2 copy-start.17
  309.1 65.0 %copy-start.15 = (bf16[4,256,2,128]{3,1,2,0:T(8,128)(2,1)}, bf16[4,256,2,128]{3,1,2,0:T(8,128)(2,1)S(1)}, u32[]{:S(2)}) copy-start(bf16[4,256,2,128]{3,1,2,0:T(8,128)(2,1)S(1)} %fusion.58) | copy-start | bytes 1572868
  367.2 7.5 copy-start.34
  374.7 23.1 %copy-start.43 = (f32[128]{0:T(128)}, f32[128]{0:T(128)S(1)}, u32[]{:S(2)}) copy-start(f32[128]{0:T(128)S(1)} %add_rsqrt_fusion.2) | copy-start | bytes 1540
  375.7 229.7 %all-gather.28.cloned.1.call-start = ((), (), s32[]{:S(2)}) async-start(), calls=%async_computation.19 | async-start | bytes 11943936 | tf_op jit(solution)/shard_map/all_gather | solution.py:123
  397.7 308.0 %all-gather.30.cloned.1.call-start = ((), (), s32[]{:S(2)}) async-start(), calls=%async_computation.20 | async-start | bytes 11943936 | tf_op jit(solution)/shard_map/all_gather | solution.py:124
  418.8 336.4 %reduce-scatter.9.cloned.1.call-start = ((), (), s32[]{:S(2)}) async-start(), calls=%async_computation.21 | async-start | bytes 2949120 | tf_op jit(solution)/shard_map/reduce_scatter | solution.py:134
  705.7 50.8 %copy-start.11 = (bf16[1,2,64,2304]{3,2,1,0:T(8,128)(2,1)S(1)}, bf16[1,2,64,2304]{3,2,1,0:T(8,128)(2,1)}, u32[]{:S(2)}) copy-start(bf16[1,2,64,2304]{3,2,1,0:T(8,128)(2,1)} %param.21) | copy-start | bytes 1769476
  705.7 50.8 %copy-start.33 = (f32[2304]{0:T(1024)S(1)}, f32[2304]{0:T(1024)}, u32[]{:S(2)}) copy-start(f32[2304]{0:T(1024)} %get-tuple-element.58) | copy-start | bytes 27652
  717.1 81.3 %all-gather.32.cloned.1.call-start = ((), (), s32[]{:S(2)}) async-start(), calls=%async_computation.22 | async-start | bytes 2949120 | tf_op jit(solution)/shard_map/all_gather | solution.py:143
  756.5 56.2 %copy-start.42 = (f32[128]{0:T(128)}, f32[128]{0:T(128)S(1)}, u32[]{:S(2)}) copy-start(f32[128]{0:T(128)S(1)} %add_rsqrt_fusion.1) | copy-start | bytes 1540
  760.9 110.1 %reduce-scatter.11.cloned.1.call-start = ((), (), s32[]{:S(2)}) async-start(), calls=%async_computation.23 | async-start | bytes 2949120 | tf_op jit(solution)/shard_map/reduce_scatter | solution.py:151
  812.6 9.9 copy-start.52
  812.6 9.9 copy-start.53
  833.4 39.7 %copy-start.6 = (bf16[128,2304]{1,0:T(8,128)(2,1)S(1)}, bf16[128,2304]{1,0:T(8,128)(2,1)}, u32[]{:S(2)}) copy-start(bf16[128,2304]{1,0:T(8,128)(2,1)} %reduce-scatter.9.cloned.1.call-done) | copy-start | bytes 1769476
  833.5 206.1 %reduce-scatter.13.cloned.1.call-start = ((), (), s32[]{:S(2)}) async-start(), calls=%async_computation.24 | async-start | bytes 2359296 | tf_op jit(solution)/shard_map/reduce_scatter | solution.py:232
  835.0 42.5 %copy-start.47 = (f32[128]{0:T(128)S(1)}, f32[128]{0:T(128)}, u32[]{:S(2)}) copy-start(f32[128]{0:T(128)} %copy-done.46) | copy-start | bytes 1540
  903.8 10.8 copy-start.50
  903.8 142.3 %reduce-scatter.15.cloned.1.call-start = ((), (), s32[]{:S(2)}) async-start(), calls=%async_computation.25 | async-start | bytes 2359296 | tf_op jit(solution)/shard_map/reduce_scatter | solution.py:238
  904.1 10.5 copy-start.54
  914.6 8.3 copy-start.13
  931.4 381.3 %reduce-scatter.17.cloned.1.call-start = ((), (), s32[]{:S(2)}) async-start(), calls=%async_computation.26 | async-start | bytes 35831808 | tf_op jit(solution)/shard_map/reduce_scatter | solution.py:155
  1003.0 1129.3 %all-reduce.3.cloned.1.call-start = ((), (), s32[]{:S(2)}) async-start(), calls=%async_computation.27 | async-start | bytes 113393664
  1005.5 10.2 copy-start.20
  1005.5 10.2 copy-start.23
  1023.4 8.0 copy-start.1
  1031.4 9.4 copy-start.24
  1190.5 130.8 %copy-start.49 = (f32[128]{0:T(128)S(1)}, f32[128]{0:T(128)}, u32[]{:S(2)}) copy-start(f32[128]{0:T(128)} %get-tuple-element.55) | copy-start | bytes 1540
  1316.9 37.5 %copy-start.5 = (f32[128,2304]{1,0:T(8,128)S(1)}, f32[128,2304]{1,0:T(8,128)}, u32[]{:S(2)}) copy-start(f32[128,2304]{1,0:T(8,128)} %copy-done.4) | copy-start | bytes 3538948
  1316.9 33.2 %all-to-all-start.5 = ((bf16[4,72,2304]{2,1,0:T(8,128)(2,1)}), bf16[4,72,2304]{2,1,0:T(8,128)(2,1)}, u32[]{:S(2)}, u32[]{:S(2)}) async-start(bf16[4,72,2304]{2,1,0:T(8,128)(2,1)} %bitcast.276), calls=%async_computation.9 | async-start | bytes 2654208 | tf_op jit(solution)/shard_map/all_to_all | solution.py:189
  1350.1 792.5 %all-to-all-start.3 = ((bf16[4,72,2304]{2,1,0:T(8,128)(2,1)}), bf16[4,72,2304]{2,1,0:T(8,128)(2,1)}, u32[]{:S(2)}, u32[]{:S(2)}) async-start(bf16[4,72,2304]{2,1,0:T(8,128)(2,1)} %bitcast.275), calls=%async_computation.7 | async-start | bytes 2654208 | tf_op jit(solution)/shard_map/all_to_all | solution.py:175
  2142.5 19.6 all-to-all-start.4
  (27 other events, 93.4 us)
Sparse Core Ops, SparseCore 0:
  10.9 64.9 all-gather.15
  78.8 61.7 all-gather.11
  142.8 27.5 all-gather.17
  172.4 28.5 all-gather.13
  203.7 80.6 all-gather.19
  287.2 79.9 all-gather.21
  368.8 96.2 all-gather.25
  467.5 37.9 all-gather.23
  507.1 98.2 all-gather.27
  606.9 98.7 all-gather.29
  717.2 37.9 reduce-scatter.8
  761.0 37.3 all-gather.31
  833.6 37.3 reduce-scatter.10
  903.9 30.4 reduce-scatter.12
  937.1 34.5 reduce-scatter.14
  1003.2 309.5 reduce-scatter.16
  1319.0 813.3 all-reduce.2
where the time goes:
time: 2190 us; the launch traced here: 2170 us
  waiting for transfers between devices  1590 us (73%)
  local copies, waits for them, and re-layouts  241 us (11%)
  matrix products  199 us (9%)
  blocking collectives  60.3 us (3%)
  other arithmetic  48.2 us (2%)
    unnamed x18, waiting for transfers between devices  779 us
    concatenate x1, local copies, waits for them, and re-layouts, local(): jnp.concatenate([lax.dot_general(attn_in, grad_q_low, CONTRACT_FIRST, pre...  129 us
    reduce_scatter x1, waiting for transfers between devices, local(): lax.psum_scatter(jnp.concatenate([lax.dot_general(group_in, grad_gate_low...  122 us
    all_gather x1, waiting for transfers between devices, local(): lax.all_gather(relayed[1], 'cp', axis=0, tiled=True)  88.3 us
    all_gather x1, waiting for transfers between devices, local(): lax.all_gather(relayed[2], 'cp', axis=0, tiled=True)  87.5 us
    all_gather x1, waiting for transfers between devices, local(): lax.all_gather(w_query, ('cp', 'fsdp'), axis=0, tiled=True)  80.1 us
    all_gather x1, waiting for transfers between devices, local(): lax.all_gather(w_key, ('cp', 'fsdp'), axis=0, tiled=True)  61.1 us
    all_gather x1, waiting for transfers between devices, local(): lax.all_gather(w_out, ('cp', 'fsdp'), axis=0, tiled=True)  58 us
  transfers between devices with their start and end apart: 20, of which 17 were waited for; matrix products, arithmetic and copies ran while one was open for 18% of the time, Pallas kernels for 0%

commit v1 on v0

--- a/solution.py
+++ b/solution.py
@@ -300,9 +300,220 @@
     )
 
 
+def weights_in(shard):
+    pieces = lax.all_to_all(shard, "cp", split_axis=1, concat_axis=0, tiled=False)
+    rows, ranks, columns = shard.shape
+    whole = lax.all_gather(pieces.reshape(-1, columns), "fsdp", axis=0, tiled=True)
+    whole = whole.reshape(-1, ranks, rows, columns).transpose(1, 0, 2, 3)
+    return whole.reshape(-1, columns)
+
+
+def weights_out(grads, ranks, planes):
+    rows = grads.shape[0] // (ranks * planes)
+    parted = grads.astype(jnp.bfloat16).reshape(ranks, planes, rows, grads.shape[1])
+    parted = parted.transpose(1, 0, 2, 3).reshape(grads.shape)
+    sums = lax.psum_scatter(parted, "fsdp", scatter_dimension=0, tiled=True)
+    return lax.all_to_all(
+        sums.reshape(ranks, rows, -1), "cp", split_axis=0, concat_axis=1, tiled=False
+    )
+
+
+def by_heads(
+    tokens, gains, w_query, w_key, w_value, w_out, w_gate, w_up, w_down, order, cotangent
+):
+    width = tokens.shape[-1]
+    span = tokens.shape[2]
+    rows = w_query.shape[0]
+    ranks = lax.axis_size("cp")
+    planes = lax.axis_size("fsdp")
+    scale_q = HEAD ** (-0.5)
+    rank = lax.axis_index("cp")
+    even = rank % 2 == 0
+    offsets = jnp.arange(span, dtype=jnp.int32)
+    positions = (order[:, None] * span + offsets[None, :]).reshape(-1)
+    visible = positions[None, :] <= positions[:, None]
+    inverse = jnp.exp(-math.log(ROPE_BASE) * jnp.arange(HEAD // 2, dtype=jnp.float32) * 2.0 / HEAD)
+    angle = positions.astype(jnp.float32)[:, None] * inverse[None, :]
+    cosine = jnp.cos(angle)
+    sine = jnp.sin(angle)
+    mixed_cos = jnp.where(even, cosine, 1.0)
+    mixed_sin = jnp.where(even, sine, 0.0)
+
+    def turn(values, cos_t, sin_t):
+        middle = values.shape[-1] // 2
+        first = values[:, :middle]
+        second = values[:, middle:]
+        return jnp.concatenate(
+            [first * cos_t - second * sin_t, second * cos_t + first * sin_t], axis=-1
+        )
+
+    swap = [(i, i ^ 1) for i in range(ranks)]
+    hidden = tokens.reshape(-1, width).astype(jnp.float32)
+    normed_one, factor_one = normalize(hidden)
+    attn_in = (normed_one * gains[0]).astype(jnp.bfloat16)
+    seq_in = lax.all_gather(attn_in, "cp", axis=0, tiled=True)
+    pairs = jnp.stack(
+        [w_key.reshape(rows, KV_HEADS, HEAD), w_value.reshape(rows, KV_HEADS, HEAD)], axis=2
+    ).reshape(rows, ranks, HEAD)
+    attn_w = weights_in(
+        jnp.concatenate(
+            [w_query.reshape(rows, ranks, HEAD), pairs, w_out.reshape(rows, ranks, HEAD)], axis=-1
+        )
+    )
+    w_lin = attn_w[:, : 2 * HEAD]
+    w_back = attn_w[:, 2 * HEAD :]
+    lin = jnp.dot(seq_in, w_lin, preferred_element_type=jnp.float32)
+    query = turn(lin[:, :HEAD], cosine, sine).astype(jnp.bfloat16)
+    mixed = turn(lin[:, HEAD:], mixed_cos, mixed_sin).astype(jnp.bfloat16)
+    other = lax.ppermute(mixed, "cp", swap)
+    keys = jnp.where(even, mixed, other)
+    values = jnp.where(even, other, mixed)
+    raw = lax.dot_general(query, keys, CONTRACT_LAST, preferred_element_type=jnp.float32) * scale_q
+    bent = jnp.tanh(raw / SOFT_CAP)
+    scores = jnp.where(visible, SOFT_CAP * bent, -1e30)
+    top_score = jnp.max(scores, axis=-1, keepdims=True)
+    expo = jnp.exp(scores - top_score)
+    total_mass = jnp.sum(expo, axis=-1, keepdims=True)
+    probs_full = expo / total_mass
+    probs_low = probs_full.astype(jnp.bfloat16)
+    attended_low = jnp.dot(probs_low, values, preferred_element_type=jnp.float32).astype(
+        jnp.bfloat16
+    )
+    share_attn = lax.dot_general(
+        attended_low, w_back, CONTRACT_LAST, preferred_element_type=jnp.float32
+    )
+    attn_out = lax.psum_scatter(
+        share_attn.astype(jnp.bfloat16), "cp", scatter_dimension=0, tiled=True
+    ).astype(jnp.float32)
+    normed_two, factor_two = normalize(attn_out)
+    middle_sum = hidden + normed_two * gains[1]
+    normed_three, factor_three = normalize(middle_sum)
+    ffn_in = (normed_three * gains[2]).astype(jnp.bfloat16)
+    gate_part, up_part, down_part = (
+        weights_in(piece.reshape(rows, ranks, -1)) for piece in (w_gate, w_up, w_down)
+    )
+    group_in = lax.all_gather(ffn_in, "cp", axis=0, tiled=True)
+    gate = jnp.dot(group_in, gate_part, preferred_element_type=jnp.float32)
+    upper = jnp.dot(group_in, up_part, preferred_element_type=jnp.float32)
+    activated = jax.nn.gelu(gate, approximate=True)
+    inner_low = (activated * upper).astype(jnp.bfloat16)
+    share_out = lax.dot_general(
+        inner_low, down_part, CONTRACT_LAST, preferred_element_type=jnp.float32
+    )
+    ffn_out = lax.psum_scatter(
+        share_out.astype(jnp.bfloat16), "cp", scatter_dimension=0, tiled=True
+    ).astype(jnp.float32)
+    normed_four, factor_four = normalize(ffn_out)
+    result = middle_sum + normed_four * gains[3]
+    output = result.astype(jnp.bfloat16).reshape(tokens.shape)
+    grad_result = cotangent.reshape(-1, width).astype(jnp.float32)
+    gain_four = jnp.sum(grad_result * normed_four, axis=0)
+    grad_ffn_low = norm_back(grad_result * gains[3], normed_four, factor_four).astype(jnp.bfloat16)
+    group_grad = lax.all_gather(grad_ffn_low, "cp", axis=0, tiled=True)
+    grad_inner = jnp.dot(group_grad, down_part, preferred_element_type=jnp.float32)
+    unused_value, gelu_back = jax.vjp(partial(jax.nn.gelu, approximate=True), gate)
+    grad_gate_low = gelu_back(grad_inner * upper)[0].astype(jnp.bfloat16)
+    grad_upper_low = (grad_inner * activated).astype(jnp.bfloat16)
+    share_in = lax.dot_general(
+        grad_gate_low, gate_part, CONTRACT_LAST, preferred_element_type=jnp.float32
+    ) + lax.dot_general(grad_upper_low, up_part, CONTRACT_LAST, preferred_element_type=jnp.float32)
+    grad_ffn_in = lax.psum_scatter(
+        share_in.astype(jnp.bfloat16), "cp", scatter_dimension=0, tiled=True
+    ).astype(jnp.float32)
+    grad_gate, grad_up, grad_down = (
+        weights_out(
+            lax.dot_general(left, right, CONTRACT_FIRST, preferred_element_type=jnp.float32),
+            ranks,
+            planes,
+        )
+        .astype(jnp.float32)
+        .reshape(rows, -1)
+        for left, right in (
+            (group_in, grad_gate_low),
+            (group_in, grad_upper_low),
+            (group_grad, inner_low),
+        )
+    )
+    gain_three = jnp.sum(grad_ffn_in * normed_three, axis=0)
+    grad_middle = grad_result + norm_back(grad_ffn_in * gains[2], normed_three, factor_three)
+    gain_two = jnp.sum(grad_middle * normed_two, axis=0)
+    grad_attn_low = norm_back(grad_middle * gains[1], normed_two, factor_two).astype(jnp.bfloat16)
+    seq_grad = lax.all_gather(grad_attn_low, "cp", axis=0, tiled=True)
+    grad_att_low = jnp.dot(seq_grad, w_back, preferred_element_type=jnp.float32).astype(
+        jnp.bfloat16
+    )
+    grad_probs = lax.dot_general(
+        grad_att_low, values, CONTRACT_LAST, preferred_element_type=jnp.float32
+    )
+    delta = jnp.sum(grad_probs * probs_full, axis=-1, keepdims=True)
+    grad_raw = (probs_full * (grad_probs - delta) * (1.0 - bent * bent)).astype(jnp.bfloat16)
+    grad_query = jnp.dot(grad_raw, keys, preferred_element_type=jnp.float32) * scale_q
+    grad_keys = (
+        lax.dot_general(grad_raw, query, CONTRACT_FIRST, preferred_element_type=jnp.float32)
+        * scale_q
+    )
+    grad_values = lax.dot_general(
+        probs_low, grad_att_low, CONTRACT_FIRST, preferred_element_type=jnp.float32
+    )
+    grad_mixed = jnp.where(even, grad_keys, grad_values) + lax.ppermute(
+        jnp.where(even, grad_values, grad_keys), "cp", swap
+    )
+    grad_lin = jnp.concatenate(
+        [
+            turn(grad_query, cosine, -sine).astype(jnp.bfloat16),
+            turn(grad_mixed, mixed_cos, -mixed_sin).astype(jnp.bfloat16),
+        ],
+        axis=1,
+    )
+    share_back = lax.dot_general(
+        grad_lin, w_lin, CONTRACT_LAST, preferred_element_type=jnp.float32
+    )
+    grad_attn_in = lax.psum_scatter(
+        share_back.astype(jnp.bfloat16), "cp", scatter_dimension=0, tiled=True
+    ).astype(jnp.float32)
+    attn_sums = weights_out(
+        jnp.concatenate(
+            [
+                lax.dot_general(
+                    seq_in, grad_lin, CONTRACT_FIRST, preferred_element_type=jnp.float32
+                ),
+                lax.dot_general(
+                    seq_grad, attended_low, CONTRACT_FIRST, preferred_element_type=jnp.float32
+                ),
+            ],
+            axis=1,
+        ),
+        ranks,
+        planes,
+    ).astype(jnp.float32)
+    grad_wq = attn_sums[:, :, :HEAD].reshape(rows, -1)
+    grad_pairs = attn_sums[:, :, HEAD : 2 * HEAD].reshape(rows, KV_HEADS, 2, HEAD)
+    grad_wk = grad_pairs[:, :, 0].reshape(rows, -1)
+    grad_wv = grad_pairs[:, :, 1].reshape(rows, -1)
+    grad_wo = attn_sums[:, :, 2 * HEAD :].reshape(rows, -1)
+    gain_one = jnp.sum(grad_attn_in * normed_one, axis=0)
+    grad_hidden = grad_middle + norm_back(grad_attn_in * gains[0], normed_one, factor_one)
+    gain_columns = jnp.stack([gain_one, gain_two, gain_three, gain_four], axis=1)
+    grad_gains = lax.psum_scatter(
+        gain_columns, ("cp", "fsdp"), scatter_dimension=0, tiled=True
+    ).T
+    return (
+        output,
+        grad_hidden.reshape(tokens.shape),
+        grad_gains,
+        grad_wq,
+        grad_wk,
+        grad_wv,
+        grad_wo,
+        grad_gate,
+        grad_up,
+        grad_down,
+    )
+
+
 def solution(mesh):
     return jax.shard_map(
-        local,
+        by_heads if mesh.shape["cp"] == HEADS else local,
         mesh=mesh,
         in_specs=(
             P("fsdp", "cp", None, None),

time: 2190 us -> 1170 us (0.53)
  waiting for transfers between devices: 1590 us -> 705 us
  local copies, waits for them, and re-layouts: 241 us -> 52 us
  blocking collectives: 60.3 us -> 202 us
  matrix products: 199 us -> 120 us
    unnamed x18 -> x16, waiting for transfers between devices: 779 us -> 0.26 us
    all_gather x11 -> x8, waiting for transfers between devices: 578 us -> 346 us  [the longest x4 187 us: weights_in(): lax.all_gather(pieces.reshape(-1, columns), 'fsdp', axis=0, tiled=True)]
    concatenate x2 -> x1, local copies, waits for them, and re-layouts: 130 us -> 1.98 us  [by_heads(): jnp.concatenate([lax.dot_general(seq_in, grad_lin, CONTRACT_FIRST, prefer...]
    reduce_scatter x5 -> x8, waiting for transfers between devices: 196 us -> 304 us  [the longest x4 167 us: weights_out(): sums = lax.psum_scatter(parted, 'fsdp', scatter_dimension=0, tiled=True)]
    all_to_all x3 -> x4, blocking collectives: 60.3 us -> 166 us  [weights_in(): lax.all_to_all(shard, 'cp', split_axis=1, concat_axis=0, tiled=False)]
    dot_general x27 -> x21, matrix products: 199 us -> 120 us  [the longest x3 26.9 us: by_heads(): lax.dot_general(left, right, CONTRACT_FIRST, preferred_element_type=jnp.f...]
    unnamed x0 -> x1, blocking collectives: none -> 36.5 us
    unnamed x115 -> x135, local copies, waits for them, and re-layouts: 45.4 us -> 15.2 us
  transfers between devices with their start and end apart: 20 -> 22, of which waited for: 17 -> 18; matrix products, arithmetic and copies ran while one was open for 18% -> 9% of each run, Pallas kernels for 0% -> 0%
where the time goes in v1:
time: 1170 us; the launch traced here: 1160 us
  waiting for transfers between devices  705 us (60%)
  blocking collectives  202 us (17%)
  matrix products  120 us (10%)
  local copies, waits for them, and re-layouts  52 us (4%)
  other arithmetic  38.5 us (3%)
  starting transfers between devices  24.7 us (2%)
  between operations  15.5 us (1%)
    all_gather x4, waiting for transfers between devices, weights_in(): lax.all_gather(pieces.reshape(-1, columns), 'fsdp', axis=0, tiled=True)  187 us
    reduce_scatter x4, waiting for transfers between devices, weights_out(): sums = lax.psum_scatter(parted, 'fsdp', scatter_dimension=0, tiled=True)  167 us
    all_to_all x4, blocking collectives, weights_in(): lax.all_to_all(shard, 'cp', split_axis=1, concat_axis=0, tiled=False)  166 us
    reduce_scatter x1, waiting for transfers between devices, by_heads(): lax.psum_scatter(share_in.astype(jnp.bfloat16), 'cp', scatter_dimension=0...  53.5 us
    reduce_scatter x1, waiting for transfers between devices, by_heads(): lax.psum_scatter(share_out.astype(jnp.bfloat16), 'cp', scatter_dimension=...  53.5 us
    all_to_all x4, waiting for transfers between devices, weights_out(): lax.all_to_all(sums.reshape(ranks, rows, -1), 'cp', split_axis=0, concat_...  53.2 us
    all_gather x1, waiting for transfers between devices, by_heads(): group_grad = lax.all_gather(grad_ffn_low, 'cp', axis=0, tiled=True)  49.6 us
    all_gather x1, waiting for transfers between devices, by_heads(): seq_in = lax.all_gather(attn_in, 'cp', axis=0, tiled=True)  48.5 us
  transfers between devices with their start and end apart: 22, of which 18 were waited for; matrix products, arithmetic and copies ran while one was open for 9% of the time, Pallas kernels for 0%

profile of v1, /device:TPU:9, one launch (start us, length us, event | category | flops | bytes accessed | tf_op | source)
XLA Modules:
  0.0 1158.4 jit_solution(12143812199905688368)
XLA Ops:
  13.1 26.4 %all_to_all.96 = bf16[1,72,8,768]{3,1,0,2:T(8,128)(2,1)} all-to-all(bf16[1,72,8,768]{3,1,0,2:T(8,128)(2,1)S(1)} %copy.61), channel_id=1, replica_groups=mesh['cp'=8,'fsdp'=4] {'cp'}, dimensions={2} | all-to-all | bytes 1769472 | tf_op jit(solution)/shard_map/all_to_all | solution.py:304
  41.9 45.0 %all-gather.11.cloned.1.call-done = bf16[2304,768]{1,0:T(8,128)(2,1)} async-done(((bf16[576,768]{1,0:T(8,128)(2,1)}), bf16[2304,768]{1,0:T(8,128)(2,1)}) %all-gather.11.cloned.1.call-update) | async-done | bytes 3538960 | tf_op jit(solution)/shard_map/all_gather | solution.py:306
  86.9 4.1 copy.62
  91.0 48.5 %all-gather.9.cloned.1.call-done = bf16[1024,2304]{1,0:T(8,128)(2,1)} async-done(((bf16[128,2304]{1,0:T(8,128)(2,1)}), bf16[1024,2304]{1,0:T(8,128)(2,1)}) %all-gather.9.cloned.1.call-update) | async-done | bytes 4718608 | tf_op jit(solution)/shard_map/all_gather | solution.py:354
  139.5 5.3 fusion.10
  155.3 4.9 convolution_convert_fusion.5
  161.9 58.1 %all_to_all.97 = bf16[1,72,8,1152]{3,1,0,2:T(8,128)(2,1)} all-to-all(bf16[1,72,8,1152]{3,1,0,2:T(8,128)(2,1)S(1)} %copy.63), channel_id=1, replica_groups=mesh['cp'=8,'fsdp'=4] {'cp'}, dimensions={2} | all-to-all | bytes 2654208 | tf_op jit(solution)/shard_map/all_to_all | solution.py:304
  220.4 45.6 %all_to_all.98 = bf16[1,72,8,1152]{3,1,0,2:T(8,128)(2,1)} all-to-all(bf16[1,72,8,1152]{3,1,0,2:T(8,128)(2,1)S(1)} %copy.65), channel_id=1, replica_groups=mesh['cp'=8,'fsdp'=4] {'cp'}, dimensions={2} | all-to-all | bytes 2654208 | tf_op jit(solution)/shard_map/all_to_all | solution.py:304
  266.7 35.7 %all_to_all.99 = bf16[1,72,8,1152]{3,1,0,2:T(8,128)(2,1)} all-to-all(bf16[1,72,8,1152]{3,1,0,2:T(8,128)(2,1)S(1)} %copy.67), channel_id=1, replica_groups=mesh['cp'=8,'fsdp'=4] {'cp'}, dimensions={2} | all-to-all | bytes 2654208 | tf_op jit(solution)/shard_map/all_to_all | solution.py:304
  307.8 25.6 %all-gather.15.cloned.1.call-done = bf16[2304,1152]{1,0:T(8,128)(2,1)} async-done(((bf16[576,1152]{1,0:T(8,128)(2,1)}), bf16[2304,1152]{1,0:T(8,128)(2,1)}) %all-gather.15.cloned.1.call-update) | async-done | bytes 5308432 | tf_op jit(solution)/shard_map/all_gather | solution.py:306
  333.4 5.3 copy.64
  338.7 58.3 %all-gather.17.cloned.1.call-done = bf16[2304,1152]{1,0:T(8,128)(2,1)} async-done(((bf16[576,1152]{1,0:T(8,128)(2,1)}), bf16[2304,1152]{1,0:T(8,128)(2,1)}) %all-gather.17.cloned.1.call-update) | async-done | bytes 5308432 | tf_op jit(solution)/shard_map/all_gather | solution.py:306
  397.0 5.3 copy.66
  402.3 58.2 %all-gather.19.cloned.1.call-done = bf16[2304,1152]{1,0:T(8,128)(2,1)} async-done(((bf16[576,1152]{1,0:T(8,128)(2,1)}), bf16[2304,1152]{1,0:T(8,128)(2,1)}) %all-gather.19.cloned.1.call-update) | async-done | bytes 5308432 | tf_op jit(solution)/shard_map/all_gather | solution.py:306
  460.5 5.3 copy.68
  465.9 47.2 %all-gather.13.cloned.1.call-done = bf16[1024,2304]{1,0:T(8,128)(2,1)} async-done(((bf16[128,2304]{1,0:T(8,128)(2,1)}), bf16[1024,2304]{1,0:T(8,128)(2,1)}) %all-gather.13.cloned.1.call-update) | async-done | bytes 4718608 | tf_op jit(solution)/shard_map/all_gather | solution.py:395
  513.1 9.8 fusion.103
  523.0 8.3 multiply_convert_fusion.1
  532.7 7.9 convolution_convert_fusion.4
  540.7 53.5 %reduce-scatter.12.cloned.1.call-done = bf16[128,2304]{1,0:T(8,128)(2,1)} async-done(((bf16[1024,2304]{1,0:T(8,128)(2,1)}), bf16[128,2304]{1,0:T(8,128)(2,1)}) %reduce-scatter.12.cloned.1.call-update) | async-done | bytes 589840 | tf_op jit(solution)/shard_map/reduce_scatter | solution.py:403
  600.5 49.6 %all-gather.21.cloned.1.call-done = bf16[1024,2304]{1,0:T(8,128)(2,1)} async-done(((bf16[128,2304]{1,0:T(8,128)(2,1)}), bf16[1024,2304]{1,0:T(8,128)(2,1)}) %all-gather.21.cloned.1.call-update) | async-done | bytes 4718608 | tf_op jit(solution)/shard_map/all_gather | solution.py:412
  650.1 15.4 %multiply_convert_fusion = (bf16[1024,1152]{1,0:T(8,128)(2,1)}, bf16[1024,1152]{1,0:T(8,128)(2,1)S(1)}) fusion(f32[1024,1152]{1,0:T(8,128)} %copy-done.49, f32[1024,1152]{1,0:T(8,128)} %get-tuple-element.44, bf16[1024,2304]{1,0:T(8,128)(2,1)} %all-gather.21.cloned.1.call-done, bf16[2304,1152]{1,0:T(8,128)(2,1)} %bitcast.234), kind=kOutput, calls=%fused_computation.16 | convolution fusion | flops 5464129536 | bytes 24182784 | tf_op jit(solution)/shard_map/dot_general | solution.py:413
  665.5 6.3 fusion.104
  671.8 10.9 add_convert_fusion
  682.9 53.5 %reduce-scatter.14.cloned.1.call-done = bf16[128,2304]{1,0:T(8,128)(2,1)} async-done(((bf16[1024,2304]{1,0:T(8,128)(2,1)}), bf16[128,2304]{1,0:T(8,128)(2,1)}) %reduce-scatter.14.cloned.1.call-update) | async-done | bytes 589840 | tf_op jit(solution)/shard_map/reduce_scatter | solution.py:420
  738.7 3.7 fusion.36
  743.9 9.0 convolution_convert_fusion
  752.8 2.8 copy.82
  755.7 9.0 convolution_convert_fusion.2
  764.7 2.8 copy.76
  767.6 9.0 convolution_convert_fusion.1
  776.6 2.9 copy.79
  779.8 13.9 %all-gather.23.cloned.1.call-done = bf16[1024,2304]{1,0:T(8,128)(2,1)} async-done(((bf16[128,2304]{1,0:T(8,128)(2,1)}), bf16[1024,2304]{1,0:T(8,128)(2,1)}) %all-gather.23.cloned.1.call-update) | async-done | bytes 4718608 | tf_op jit(solution)/shard_map/all_gather | solution.py:441
  793.7 4.2 convolution_convert_fusion.8
  811.7 3.7 convolution_convert_fusion.6
  817.7 40.3 %reduce-scatter.24.cloned.1.call-done = bf16[576,1152]{1,0:T(8,128)(2,1)} async-done(((bf16[2304,1152]{1,0:T(8,128)(2,1)}), bf16[576,1152]{1,0:T(8,128)(2,1)}) %reduce-scatter.24.cloned.1.call-update) | async-done | bytes 1327120 | tf_op jit(solution)/shard_map/reduce_scatter | solution.py:315
  858.1 5.6 all-to-all-start.7
  863.7 6.7 convolution_convert_fusion.3
  870.5 52.5 %reduce-scatter.20.cloned.1.call-done = bf16[576,1152]{1,0:T(8,128)(2,1)} async-done(((bf16[2304,1152]{1,0:T(8,128)(2,1)}), bf16[576,1152]{1,0:T(8,128)(2,1)}) %reduce-scatter.20.cloned.1.call-update) | async-done | bytes 1327120 | tf_op jit(solution)/shard_map/reduce_scatter | solution.py:315
  923.0 5.6 all-to-all-start.5
  928.6 59.2 %reduce-scatter.22.cloned.1.call-done = bf16[576,1152]{1,0:T(8,128)(2,1)} async-done(((bf16[2304,1152]{1,0:T(8,128)(2,1)}), bf16[576,1152]{1,0:T(8,128)(2,1)}) %reduce-scatter.22.cloned.1.call-update) | async-done | bytes 1327120 | tf_op jit(solution)/shard_map/reduce_scatter | solution.py:315
  987.8 5.6 all-to-all-start.6
  993.4 29.0 %all-to-all-done.6 = bf16[8,72,1,1152]{3,1,2,0:T(8,128)(2,1)} async-done(((bf16[8,72,1,1152]{3,1,2,0:T(8,128)(2,1)}), bf16[8,72,1,1152]{3,1,2,0:T(8,128)(2,1)}, u32[]{:S(2)}, u32[]{:S(2)}) %all-to-all-start.6) | async-done | bytes 1327136 | tf_op jit(solution)/shard_map/all_to_all | solution.py:316
  1022.4 15.5 %reduce-scatter.18.cloned.1.call-done = bf16[576,768]{1,0:T(8,128)(2,1)} async-done(((bf16[2304,768]{1,0:T(8,128)(2,1)}), bf16[576,768]{1,0:T(8,128)(2,1)}) %reduce-scatter.18.cloned.1.call-update) | async-done | bytes 884752 | tf_op jit(solution)/shard_map/reduce_scatter | solution.py:315
  1037.9 5.6 all-to-all-start.4
  1051.8 24.2 %all-to-all-done.4 = bf16[8,72,1,768]{3,1,2,0:T(8,128)(2,1)} async-done(((bf16[8,72,1,768]{3,1,2,0:T(8,128)(2,1)}), bf16[8,72,1,768]{3,1,2,0:T(8,128)(2,1)}, u32[]{:S(2)}, u32[]{:S(2)}) %all-to-all-start.4) | async-done | bytes 884768 | tf_op jit(solution)/shard_map/all_to_all | solution.py:316
  1081.1 29.1 %reduce-scatter.16.cloned.1.call-done = bf16[128,2304]{1,0:T(8,128)(2,1)} async-done(((bf16[1024,2304]{1,0:T(8,128)(2,1)}), bf16[128,2304]{1,0:T(8,128)(2,1)}) %reduce-scatter.16.cloned.1.call-update) | async-done | bytes 589840 | tf_op jit(solution)/shard_map/reduce_scatter | solution.py:471
  1111.8 36.5 %all-reduce = f32[2304,4]{0,1:T(4,128)S(1)} all-reduce(f32[2304,4]{0,1:T(4,128)S(1)} %pad_maximum_fusion.9), channel_id=6, replica_groups=mesh['cp'=8,'fsdp'=4] {'cp','fsdp'}, use_global_device_ids=true, to_apply=%region_19.20.clone | all-reduce | flops 9216 | bytes 73728
  (245 shorter events, 72.4 us)
Async XLA Ops:
  7.2 79.7 %all-gather.11.cloned.1.call-start = ((), (), s32[]{:S(2)}) async-start(), calls=%async_computation.17 | async-start | bytes 4423680 | tf_op jit(solution)/shard_map/all_gather | solution.py:306
  11.8 27.8 %copy-start = (bf16[1,2,64,2304]{3,2,1,0:T(8,128)(2,1)S(1)}, bf16[1,2,64,2304]{3,2,1,0:T(8,128)(2,1)}, u32[]{:S(2)}) copy-start(bf16[1,2,64,2304]{3,2,1,0:T(8,128)(2,1)} %param.11) | copy-start | bytes 1769476
  12.9 27.0 %copy-start.32 = (f32[4,2304]{1,0:T(4,128)S(1)}, f32[4,2304]{1,0:T(4,128)}, u32[]{:S(2)}) copy-start(f32[4,2304]{1,0:T(4,128)} %param.12) | copy-start | bytes 110596
  12.9 28.8 %copy-start.48 = (s32[16]{0:T(128)S(1)}, s32[16]{0:T(128)}, u32[]{:S(2)}) copy-start(s32[16]{0:T(128)} %param.20) | copy-start | bytes 196
  39.5 99.9 %all-gather.9.cloned.1.call-start = ((), (), s32[]{:S(2)}) async-start(), calls=%async_computation.16 | async-start | bytes 5308416 | tf_op jit(solution)/shard_map/all_gather | solution.py:354
  39.9 51.1 %copy-start.39 = (f32[128]{0:T(128)}, f32[128]{0:T(128)S(1)}, u32[]{:S(2)}) copy-start(f32[128]{0:T(128)S(1)} %rsqrt.36) | copy-start | bytes 1540
  40.0 265.4 %copy-start.25 = (f32[2304]{0:T(1024)}, f32[2304]{0:T(1024)S(1)}, u32[]{:S(2)}) copy-start(f32[2304]{0:T(1024)S(1)} %get-tuple-element.21) | copy-start | bytes 27652
  40.0 557.7 %copy-start.24 = (f32[2304]{0:T(1024)}, f32[2304]{0:T(1024)S(1)}, u32[]{:S(2)}) copy-start(f32[2304]{0:T(1024)S(1)} %get-tuple-element.18) | copy-start | bytes 27652
  41.7 260.8 %reduce-scatter.10.cloned.1.call-start = ((), (), s32[]{:S(2)}) async-start(), calls=%async_computation.18 | async-start | bytes 5308416 | tf_op jit(solution)/shard_map/reduce_scatter | solution.py:385
  41.9 102.9 %copy-start.30 = (f32[1024]{0:T(1024)}, f32[1024]{0:T(1024)S(1)}, u32[]{:S(2)}) copy-start(f32[1024]{0:T(1024)S(1)} %convert_element_type.152) | copy-start | bytes 12292
  41.9 102.9 %copy-start.43 = (f32[128]{0:T(128)}, f32[128]{0:T(128)S(1)}, u32[]{:S(2)}) copy-start(f32[128]{0:T(128)S(1)} %multiply_exponential_fusion) | copy-start | bytes 1540
  147.3 2.0 collective-permute-start
  160.2 173.2 %all-gather.15.cloned.1.call-start = ((), (), s32[]{:S(2)}) async-start(), calls=%async_computation.20 | async-start | bytes 6635520 | tf_op jit(solution)/shard_map/all_gather | solution.py:306
  161.7 58.3 %copy-start.7 = (bf16[72,9216]{1,0:T(8,128)(2,1)S(1)}, bf16[72,9216]{1,0:T(8,128)(2,1)}, u32[]{:S(2)}) copy-start(bf16[72,9216]{1,0:T(8,128)(2,1)} %param.18) | copy-start | bytes 3981316
  220.0 177.0 %all-gather.17.cloned.1.call-start = ((), (), s32[]{:S(2)}) async-start(), calls=%async_computation.21 | async-start | bytes 6635520 | tf_op jit(solution)/shard_map/all_gather | solution.py:306
  220.3 46.0 %copy-start.8 = (bf16[72,9216]{1,0:T(8,128)(2,1)S(1)}, bf16[72,9216]{1,0:T(8,128)(2,1)}, u32[]{:S(2)}) copy-start(bf16[72,9216]{1,0:T(8,128)(2,1)} %param.19) | copy-start | bytes 3981316
  266.0 194.5 %all-gather.19.cloned.1.call-start = ((), (), s32[]{:S(2)}) async-start(), calls=%async_computation.22 | async-start | bytes 6635520 | tf_op jit(solution)/shard_map/all_gather | solution.py:306
  302.4 210.7 %all-gather.13.cloned.1.call-start = ((), (), s32[]{:S(2)}) async-start(), calls=%async_computation.19 | async-start | bytes 5308416 | tf_op jit(solution)/shard_map/all_gather | solution.py:395
  303.7 432.7 %copy-start.37 = (f32[128]{0:T(128)}, f32[128]{0:T(128)S(1)}, u32[]{:S(2)}) copy-start(f32[128]{0:T(128)S(1)} %add_rsqrt_fusion.3) | copy-start | bytes 1540
  305.4 431.0 %copy-start.42 = (f32[128]{0:T(128)}, f32[128]{0:T(128)S(1)}, u32[]{:S(2)}) copy-start(f32[128]{0:T(128)S(1)} %add_rsqrt_fusion.2) | copy-start | bytes 1540
  307.7 286.6 %reduce-scatter.12.cloned.1.call-start = ((), (), s32[]{:S(2)}) async-start(), calls=%async_computation.23 | async-start | bytes 5308416 | tf_op jit(solution)/shard_map/reduce_scatter | solution.py:403
  460.5 62.4 %slice-start.2 = ((s8[5308416]{0:T(1024)(128)(4,1)}), s8[1114112]{0:T(1024)(128)(4,1)S(1)}, s32[]{:S(2)}) async-start(s8[5308416]{0:T(1024)(128)(4,1)} %bitcast.229), calls=%async_computation.34 | async-start | bytes 2228224
  513.1 19.6 %slice-start.4 = ((s8[5308416]{0:T(1024)(128)(4,1)}), s8[4194304]{0:T(1024)(128)(4,1)S(1)}, s32[]{:S(2)}) async-start(s8[5308416]{0:T(1024)(128)(4,1)} %bitcast.235), calls=%async_computation.36 | async-start | bytes 8388608
  540.7 54.9 %copy-start.5 = (bf16[1,2,64,2304]{3,2,1,0:T(8,128)(2,1)S(1)}, bf16[1,2,64,2304]{3,2,1,0:T(8,128)(2,1)}, u32[]{:S(2)}) copy-start(bf16[1,2,64,2304]{3,2,1,0:T(8,128)(2,1)} %param.21) | copy-start | bytes 1769476
  540.7 109.4 %all-gather.21.cloned.1.call-start = ((), (), s32[]{:S(2)}) async-start(), calls=%async_computation.24 | async-start | bytes 5308416 | tf_op jit(solution)/shard_map/all_gather | solution.py:412
  595.6 69.9 %copy-start.41 = (f32[128]{0:T(128)}, f32[128]{0:T(128)S(1)}, u32[]{:S(2)}) copy-start(f32[128]{0:T(128)S(1)} %add_rsqrt_fusion.1) | copy-start | bytes 1540
  597.7 67.8 %slice-start = ((s8[5308416]{0:T(1024)(128)(4,1)}), s8[1114112]{0:T(1024)(128)(4,1)S(1)}, s32[]{:S(2)}) async-start(s8[5308416]{0:T(1024)(128)(4,1)} %bitcast.225), calls=%async_computation.32 | async-start | bytes 2228224
  600.1 136.3 %reduce-scatter.14.cloned.1.call-start = ((), (), s32[]{:S(2)}) async-start(), calls=%async_computation.25 | async-start | bytes 5308416 | tf_op jit(solution)/shard_map/reduce_scatter | solution.py:420
  682.8 53.6 %copy-start.1 = (bf16[128,2304]{1,0:T(8,128)(2,1)S(1)}, bf16[128,2304]{1,0:T(8,128)(2,1)}, u32[]{:S(2)}) copy-start(bf16[128,2304]{1,0:T(8,128)(2,1)} %reduce-scatter.10.cloned.1.call-done) | copy-start | bytes 1769476
  682.8 53.6 %copy-start.26 = (f32[2304]{0:T(1024)S(1)}, f32[2304]{0:T(1024)}, u32[]{:S(2)}) copy-start(f32[2304]{0:T(1024)} %copy-done.25) | copy-start | bytes 27652
  682.8 55.9 %copy-start.4 = (bf16[128,2304]{1,0:T(8,128)(2,1)S(1)}, bf16[128,2304]{1,0:T(8,128)(2,1)}, u32[]{:S(2)}) copy-start(bf16[128,2304]{1,0:T(8,128)(2,1)} %reduce-scatter.12.cloned.1.call-done) | copy-start | bytes 1769476
  682.8 110.9 %all-gather.23.cloned.1.call-start = ((), (), s32[]{:S(2)}) async-start(), calls=%async_computation.26 | async-start | bytes 5308416 | tf_op jit(solution)/shard_map/all_gather | solution.py:441
  743.6 114.4 %reduce-scatter.24.cloned.1.call-start = ((), (), s32[]{:S(2)}) async-start(), calls=%async_computation.31 | async-start | bytes 6635520 | tf_op jit(solution)/shard_map/reduce_scatter | solution.py:315
  755.6 167.4 %reduce-scatter.20.cloned.1.call-start = ((), (), s32[]{:S(2)}) async-start(), calls=%async_computation.29 | async-start | bytes 6635520 | tf_op jit(solution)/shard_map/reduce_scatter | solution.py:315
  767.5 220.2 %reduce-scatter.22.cloned.1.call-start = ((), (), s32[]{:S(2)}) async-start(), calls=%async_computation.30 | async-start | bytes 6635520 | tf_op jit(solution)/shard_map/reduce_scatter | solution.py:315
  779.4 18.5 %copy-start.12 = (bf16[1024,128]{0,1:T(8,128)(2,1)S(1)}, bf16[1024,128]{0,1:T(8,128)(2,1)}, u32[]{:S(2)}) copy-start(bf16[1024,128]{0,1:T(8,128)(2,1)} %copy-done.11) | copy-start | bytes 786436
  779.5 258.4 %reduce-scatter.18.cloned.1.call-start = ((), (), s32[]{:S(2)}) async-start(), calls=%async_computation.28 | async-start | bytes 4423680 | tf_op jit(solution)/shard_map/reduce_scatter | solution.py:315
  805.1 3.4 collective-permute-start.1
  858.1 64.9 %all-to-all-start.7 = ((bf16[8,72,1,1152]{3,1,2,0:T(8,128)(2,1)}), bf16[8,72,1,1152]{3,1,2,0:T(8,128)(2,1)S(1)}, u32[]{:S(2)}, u32[]{:S(2)}) async-start(bf16[8,72,1,1152]{3,1,2,0:T(8,128)(2,1)} %bitcast.259), calls=%async_computation.15 | async-start | bytes 2654208 | tf_op jit(solution)/shard_map/all_to_all | solution.py:316
  863.7 246.5 %reduce-scatter.16.cloned.1.call-start = ((), (), s32[]{:S(2)}) async-start(), calls=%async_computation.27 | async-start | bytes 5308416 | tf_op jit(solution)/shard_map/reduce_scatter | solution.py:471
  870.4 122.9 %copy-start.27 = (f32[2304]{0:T(1024)S(1)}, f32[2304]{0:T(1024)}, u32[]{:S(2)}) copy-start(f32[2304]{0:T(1024)} %get-tuple-element.16) | copy-start | bytes 27652
  870.5 122.9 %copy-start.29 = (f32[2304]{0:T(1024)S(1)}, f32[2304]{0:T(1024)}, u32[]{:S(2)}) copy-start(f32[2304]{0:T(1024)} %get-tuple-element.10) | copy-start | bytes 27652
  870.5 122.9 %copy-start.28 = (f32[2304]{0:T(1024)S(1)}, f32[2304]{0:T(1024)}, u32[]{:S(2)}) copy-start(f32[2304]{0:T(1024)} %get-tuple-element.12) | copy-start | bytes 27652
  923.0 64.8 %all-to-all-start.5 = ((bf16[8,72,1,1152]{3,1,2,0:T(8,128)(2,1)}), bf16[8,72,1,1152]{3,1,2,0:T(8,128)(2,1)}, u32[]{:S(2)}, u32[]{:S(2)}) async-start(bf16[8,72,1,1152]{3,1,2,0:T(8,128)(2,1)} %bitcast.260), calls=%async_computation.11 | async-start | bytes 2654208 | tf_op jit(solution)/shard_map/all_to_all | solution.py:316
  987.8 34.6 %all-to-all-start.6 = ((bf16[8,72,1,1152]{3,1,2,0:T(8,128)(2,1)}), bf16[8,72,1,1152]{3,1,2,0:T(8,128)(2,1)}, u32[]{:S(2)}, u32[]{:S(2)}) async-start(bf16[8,72,1,1152]{3,1,2,0:T(8,128)(2,1)} %bitcast.258), calls=%async_computation.13 | async-start | bytes 2654208 | tf_op jit(solution)/shard_map/all_to_all | solution.py:316
  1037.9 38.2 %all-to-all-start.4 = ((bf16[8,72,1,768]{3,1,2,0:T(8,128)(2,1)}), bf16[8,72,1,768]{3,1,2,0:T(8,128)(2,1)}, u32[]{:S(2)}, u32[]{:S(2)}) async-start(bf16[8,72,1,768]{3,1,2,0:T(8,128)(2,1)} %bitcast.267), calls=%async_computation.9 | async-start | bytes 1769472 | tf_op jit(solution)/shard_map/all_to_all | solution.py:316
  1077.5 32.7 %copy-start.23 = (f32[2304]{0:T(1024)S(1)}, f32[2304]{0:T(1024)}, u32[]{:S(2)}) copy-start(f32[2304]{0:T(1024)} %copy-done.22) | copy-start | bytes 27652
  1077.5 32.7 %copy-start.40 = (f32[128]{0:T(128)S(1)}, f32[128]{0:T(128)}, u32[]{:S(2)}) copy-start(f32[128]{0:T(128)} %copy-done.39) | copy-start | bytes 1540
  (36 other events, 217.9 us)
Sparse Core Ops, SparseCore 0:
  39.7 47.2 all-gather.10
  89.1 50.3 all-gather.8
  160.3 110.4 reduce-scatter.9
  272.5 60.8 all-gather.14
  335.1 61.8 all-gather.16
  398.6 61.8 all-gather.18
  462.7 50.3 all-gather.12
  540.8 53.4 reduce-scatter.11
  600.2 49.8 all-gather.20
  682.9 53.4 reduce-scatter.13
  743.8 49.8 all-gather.22
  796.5 61.5 reduce-scatter.23
  861.1 61.8 reduce-scatter.19
  925.8 61.8 reduce-scatter.21
  990.7 47.1 reduce-scatter.17
  1040.0 70.0 reduce-scatter.15

commit v2 on v1

--- a/solution.py
+++ b/solution.py
@@ -4,6 +4,8 @@
 import jax
 import jax.numpy as jnp
 from jax import lax
+from jax.experimental import pallas as pl
+from jax.experimental.pallas import tpu as pltpu
 from jax.sharding import PartitionSpec as P
 
 HEADS = 8
@@ -300,12 +302,492 @@
     )
 
 
-def weights_in(shard):
-    pieces = lax.all_to_all(shard, "cp", split_axis=1, concat_axis=0, tiled=False)
-    rows, ranks, columns = shard.shape
-    whole = lax.all_gather(pieces.reshape(-1, columns), "fsdp", axis=0, tiled=True)
-    whole = whole.reshape(-1, ranks, rows, columns).transpose(1, 0, 2, 3)
-    return whole.reshape(-1, columns)
+MESH_IDS = pl.DeviceIdType.MESH
+DMA = pltpu.SemaphoreType.DMA
+
+
+def remote(source, target, send, recv, **ids):
+    return pltpu.make_async_remote_copy(
+        src_ref=source,
+        dst_ref=target,
+        send_sem=send,
+        recv_sem=recv,
+        device_id=ids,
+        device_id_type=MESH_IDS,
+    )
+
+
+class Place:
+    def __init__(self, ranks):
+        self.ranks = ranks
+        self.depth = ranks // 2
+        self.rank = lax.axis_index("cp")
+        self.plane = lax.axis_index("fsdp")
+        self.z = self.rank // 2
+        self.core = lax.rem(self.rank, 2)
+        self.twin = 2 * self.z + 1 - self.core
+        self.above = self.z < self.depth - 1
+        self.below = self.z > 0
+
+    def greet(self, column, planes):
+        barrier = pltpu.get_barrier_semaphore()
+
+        def signal(**ids):
+            pl.semaphore_signal(barrier, inc=1, device_id=ids, device_id_type=MESH_IDS)
+
+        count = 0
+        if column:
+            for step in range(1, self.ranks):
+                signal(cp=lax.rem(self.rank + step, self.ranks))
+            count = self.ranks - 1
+        else:
+            signal(cp=self.twin)
+
+            @pl.when(self.above)
+            def _():
+                signal(cp=self.rank + 2)
+
+            @pl.when(self.below)
+            def _():
+                signal(cp=self.rank - 2)
+
+            count = (
+                1
+                + jnp.where(self.above, 1, 0).astype(jnp.int32)
+                + jnp.where(self.below, 1, 0).astype(jnp.int32)
+            )
+        if planes:
+            for flip in (1, 2):
+                signal(fsdp=jnp.bitwise_xor(self.plane, flip))
+            count = count + 2
+        pl.semaphore_wait(barrier, count)
+
+
+class Gather:
+    @staticmethod
+    def scratch(ranks):
+        return [DMA((3, ranks)), DMA((3, ranks)), DMA]
+
+    def __init__(self, place, source, whole, send, recv, local):
+        self.place, self.source, self.whole = place, source, whole
+        self.send, self.recv, self.local = send, recv, local
+
+    def copy(self, source, shard, way, step):
+        place = self.place
+        target = (place.rank + 2, place.rank - 2, place.twin)[way]
+        return remote(
+            source, self.whole.at[shard], self.send.at[way, step], self.recv.at[way, step], cp=target
+        )
+
+    def start(self):
+        place = self.place
+        pltpu.make_async_copy(self.source, self.whole.at[place.rank], self.local).start()
+
+        @pl.when(place.above)
+        def _():
+            self.copy(self.source, place.rank, 0, 0).start()
+
+        @pl.when(place.below)
+        def _():
+            self.copy(self.source, place.rank, 1, 0).start()
+
+        self.copy(self.source, place.rank, 2, 0).start()
+
+    def relay(self, step):
+        place = self.place
+        last = place.depth - 1
+
+        @pl.when(place.z >= step)
+        def _():
+            shard = place.rank - 2 * step
+            self.copy(self.whole.at[shard], shard, 0, step - 1).wait_recv()
+
+            @pl.when(place.above)
+            def _():
+                self.copy(self.whole.at[shard], shard, 0, step).start()
+
+            self.copy(self.whole.at[shard], shard, 2, step).start()
+
+        @pl.when(place.z + step <= last)
+        def _():
+            shard = place.rank + 2 * step
+            self.copy(self.whole.at[shard], shard, 1, step - 1).wait_recv()
+
+            @pl.when(place.below)
+            def _():
+                self.copy(self.whole.at[shard], shard, 1, step).start()
+
+            self.copy(self.whole.at[shard], shard, 2, last + step).start()
+
+    def finish(self):
+        place = self.place
+        last = place.depth - 1
+        own = self.whole.at[place.rank]
+        for step in range(place.depth):
+
+            @pl.when(jnp.logical_and(place.z >= step, place.above))
+            def _():
+                self.copy(own, place.rank, 0, step).wait_send()
+
+            @pl.when(jnp.logical_and(place.z + step <= last, place.below))
+            def _():
+                self.copy(own, place.rank, 1, step).wait_send()
+
+            @pl.when(place.z >= step)
+            def _():
+                self.copy(own, place.rank, 2, step).wait()
+
+            if step > 0:
+
+                @pl.when(place.z + step <= last)
+                def _():
+                    self.copy(own, place.rank, 2, last + step).wait()
+
+        pltpu.make_async_copy(self.source, own, self.local).wait()
+
+
+class Scatter:
+    @staticmethod
+    def scratch(ranks, rows, width):
+        depth = ranks // 2
+        slots = pltpu.VMEM((depth, rows, width), jnp.bfloat16)
+        return [slots] * 4 + [DMA((3, depth)), DMA((3, depth))]
+
+    def __init__(self, place, parts, out, pair, rising, falling, outbox, send, recv):
+        self.place, self.parts, self.out = place, parts, out
+        self.pair, self.rising, self.falling, self.outbox = pair, rising, falling, outbox
+        self.send, self.recv = send, recv
+        rows = parts.shape[1]
+        self.tile = 16
+        self.tiles = rows // self.tile
+
+    def swap(self, target):
+        place = self.place
+        return remote(
+            self.parts.at[2 * target + 1 - place.core],
+            self.pair.at[target],
+            self.send.at[0, target],
+            self.recv.at[0, target],
+            cp=place.twin,
+        )
+
+    def hop(self, target, way):
+        box = (self.rising, self.falling)[way]
+        return remote(
+            self.outbox.at[target],
+            box.at[target],
+            self.send.at[1 + way, target],
+            self.recv.at[1 + way, target],
+            cp=self.place.rank + (2, -2)[way],
+        )
+
+    def start(self):
+        depth = self.place.depth
+        for target in sorted(range(depth), key=lambda i: -abs(2 * i - depth + 1)):
+            self.swap(target).start()
+
+    def add(self, target, boxes, store):
+        place = self.place
+
+        def body(tile, carry):
+            rows = pl.ds(pl.multiple_of(tile * self.tile, self.tile), self.tile)
+            total = self.parts[2 * target + place.core, rows].astype(jnp.float32) + self.pair[
+                target, rows
+            ].astype(jnp.float32)
+            for box in boxes:
+                total = total + box[target, rows].astype(jnp.float32)
+            store(rows, total)
+            return carry
+
+        lax.fori_loop(0, self.tiles, body, 0)
+
+    def run(self):
+        place = self.place
+
+        def send(target, way, fed):
+            self.swap(target).wait_recv()
+            box = (self.rising, self.falling)[way]
+
+            def store(rows, total):
+                self.outbox[target, rows] = total.astype(jnp.bfloat16)
+
+            @pl.when(fed)
+            def _():
+                self.hop(target, way).wait_recv()
+                self.add(target, [box], store)
+
+            @pl.when(jnp.logical_not(fed))
+            def _():
+                self.add(target, [], store)
+
+            self.hop(target, way).start()
+
+        for step in range(place.depth - 1, 0, -1):
+
+            @pl.when(place.z + step < place.depth)
+            def _():
+                send(place.z + step, 0, place.below)
+
+            @pl.when(place.z >= step)
+            def _():
+                send(place.z - step, 1, place.above)
+
+    def finish(self):
+        place = self.place
+        self.swap(place.z).wait_recv()
+
+        def store(rows, total):
+            self.out[rows] = total
+
+        def both():
+            self.hop(place.z, 0).wait_recv()
+            self.hop(place.z, 1).wait_recv()
+            self.add(place.z, [self.rising, self.falling], store)
+
+        def lower():
+            self.hop(place.z, 0).wait_recv()
+            self.add(place.z, [self.rising], store)
+
+        def upper():
+            self.hop(place.z, 1).wait_recv()
+            self.add(place.z, [self.falling], store)
+
+        pl.when(jnp.logical_and(place.below, place.above))(both)
+        pl.when(jnp.logical_and(place.below, jnp.logical_not(place.above)))(lower)
+        pl.when(jnp.logical_and(jnp.logical_not(place.below), place.above))(upper)
+        for target in range(place.depth):
+            self.swap(target).wait_send()
+
+            @pl.when(target > place.z)
+            def _():
+                self.hop(target, 0).wait_send()
+
+            @pl.when(target < place.z)
+            def _():
+                self.hop(target, 1).wait_send()
+
+
+class Exchange:
+    @staticmethod
+    def scratch(ranks, rows, columns):
+        return [
+            pltpu.VMEM((rows, columns), jnp.bfloat16),
+            DMA((ranks,)),
+            DMA((ranks,)),
+            DMA((4,)),
+            DMA((4,)),
+        ]
+
+    def __init__(self, place, shard, whole, bounce, send, recv, send_plane, recv_plane):
+        self.place, self.shard, self.whole, self.bounce = place, shard, whole, bounce
+        self.send, self.recv = send, recv
+        self.send_plane, self.recv_plane = send_plane, recv_plane
+        self.columns = whole.shape[3]
+        self.half = place.ranks // 2
+
+    def slice_of(self, target):
+        first = pl.multiple_of(target * self.columns, 128)
+        return self.shard.at[:, pl.ds(first, self.columns)]
+
+    def piece(self, step):
+        place = self.place
+        target = lax.rem(place.rank + step, place.ranks)
+        return remote(
+            self.slice_of(target),
+            self.whole.at[place.rank, place.plane],
+            self.send.at[step],
+            self.recv.at[step],
+            cp=target,
+        )
+
+    def own(self, inward):
+        place = self.place
+        if inward:
+            return pltpu.make_async_copy(self.slice_of(place.rank), self.bounce, self.send.at[0])
+        return pltpu.make_async_copy(
+            self.bounce, self.whole.at[place.rank, place.plane], self.recv.at[0]
+        )
+
+    def start(self):
+        for step in range(1, self.place.ranks):
+            self.piece(step).start()
+        self.own(True).start()
+        self.own(True).wait()
+        self.own(False).start()
+
+    def first(self, flip):
+        column = self.whole.at[:, self.place.plane]
+        return remote(
+            column,
+            column,
+            self.send_plane.at[flip - 1],
+            self.recv_plane.at[flip - 1],
+            fsdp=jnp.bitwise_xor(self.place.plane, flip),
+        )
+
+    def second(self, flip):
+        origin = jnp.bitwise_xor(self.place.plane, flip)
+        part = self.whole.at[pl.ds((flip - 1) * self.half, self.half), origin]
+        return remote(
+            part,
+            part,
+            self.send_plane.at[flip + 1],
+            self.recv_plane.at[flip + 1],
+            fsdp=jnp.bitwise_xor(self.place.plane, 3 - flip),
+        )
+
+    def spread(self):
+        self.own(False).wait()
+        for step in range(1, self.place.ranks):
+            self.piece(step).wait()
+        for flip in (1, 2):
+            self.first(flip).start()
+
+    def relay(self):
+        for flip in (1, 2):
+            self.first(flip).wait_recv()
+            self.second(flip).start()
+
+    def finish(self):
+        for flip in (1, 2):
+            self.first(flip).wait_send()
+            self.second(flip).wait()
+
+
+def split(refs, *counts):
+    groups, first = [], 0
+    for count in counts:
+        groups.append(refs[first : first + count])
+        first += count
+    return groups
+
+
+HBM_SPEC = pl.BlockSpec(memory_space=pltpu.HBM)
+VMEM_SPEC = pl.BlockSpec(memory_space=pltpu.VMEM)
+
+
+def comm_call(body, number, outs, ins, scratch, args, flops=0, **more):
+    return pl.pallas_call(
+        body,
+        out_shape=[shape for shape, spec in outs],
+        in_specs=ins,
+        out_specs=[spec for shape, spec in outs],
+        scratch_shapes=scratch,
+        compiler_params=pltpu.CompilerParams(
+            collective_id=number, has_side_effects=True, vmem_limit_bytes=62 * 1024 * 1024
+        ),
+        **more,
+    )(*args)
+
+
+def front(ranks, planes, rows_in, attn_shard, gate_shard):
+    rows, width = rows_in.shape
+    deep, columns = attn_shard.shape[0], attn_shard.shape[1] // ranks
+    wide = gate_shard.shape[1] // ranks
+
+    def body(x, wa, wg, seq, attn, gate, *scratch):
+        place = Place(ranks)
+        for_seq, for_attn, for_gate = split(scratch, 3, 5, 5)
+        gather = Gather(place, x, seq, *for_seq)
+        attn_w = Exchange(place, wa, attn, *for_attn)
+        gate_w = Exchange(place, wg, gate, *for_gate)
+        place.greet(True, True)
+        attn_w.start()
+        gather.start()
+        gather.relay(1)
+        attn_w.spread()
+        gate_w.start()
+        gather.relay(2)
+        gather.relay(3)
+        attn_w.relay()
+        gather.finish()
+        attn_w.finish()
+        gate_w.spread()
+        gate_w.relay()
+        gate_w.finish()
+
+    low = jnp.bfloat16
+    return comm_call(
+        body,
+        0,
+        [
+            (jax.ShapeDtypeStruct((ranks, rows, width), low), HBM_SPEC),
+            (jax.ShapeDtypeStruct((ranks, planes, deep, columns), low), HBM_SPEC),
+            (jax.ShapeDtypeStruct((ranks, planes, deep, wide), low), HBM_SPEC),
+        ],
+        [HBM_SPEC] * 3,
+        Gather.scratch(ranks)
+        + Exchange.scratch(ranks, deep, columns)
+        + Exchange.scratch(ranks, deep, wide),
+        (rows_in, attn_shard, gate_shard),
+    )
+
+
+def column_gather(number, ranks, planes, rows_in, shard=None):
+    rows, width = rows_in.shape
+    outs = [(jax.ShapeDtypeStruct((ranks, rows, width), jnp.bfloat16), HBM_SPEC)]
+    scratch = Gather.scratch(ranks)
+    args = [rows_in]
+    if shard is not None:
+        deep, wide = shard.shape[0], shard.shape[1] // ranks
+        outs.append((jax.ShapeDtypeStruct((ranks, planes, deep, wide), jnp.bfloat16), HBM_SPEC))
+        scratch = scratch + Exchange.scratch(ranks, deep, wide)
+        args.append(shard)
+    count = len(args)
+
+    def body(*refs):
+        ins, made, mine, rest = split(refs, count, count, 3, 5)
+        place = Place(ranks)
+        gather = Gather(place, ins[0], made[0], *mine)
+        place.greet(shard is not None, shard is not None)
+        if shard is not None:
+            weight = Exchange(place, ins[1], made[1], *rest)
+            weight.start()
+        gather.start()
+        gather.relay(1)
+        if shard is not None:
+            weight.spread()
+        gather.relay(2)
+        gather.relay(3)
+        gather.finish()
+        if shard is not None:
+            weight.relay()
+            weight.finish()
+
+    return comm_call(body, number, outs, [HBM_SPEC] * count, scratch, args)
+
+
+def column_scatter(number, ranks, planes, parts, shard=None):
+    rows, width = parts.shape[0] // ranks, parts.shape[1]
+    outs = [(jax.ShapeDtypeStruct((rows, width), jnp.float32), VMEM_SPEC)]
+    scratch = Scatter.scratch(ranks, rows, width)
+    args = [parts.reshape(ranks, rows, width)]
+    ins = [VMEM_SPEC]
+    if shard is not None:
+        deep, wide = shard.shape[0], shard.shape[1] // ranks
+        outs.append((jax.ShapeDtypeStruct((ranks, planes, deep, wide), jnp.bfloat16), HBM_SPEC))
+        scratch = scratch + Exchange.scratch(ranks, deep, wide)
+        args.append(shard)
+        ins.append(HBM_SPEC)
+    count = len(args)
+
+    def body(*refs):
+        given, made, mine, rest = split(refs, count, count, 6, 5)
+        place = Place(ranks)
+        scatter = Scatter(place, given[0], made[0], *mine)
+        place.greet(shard is not None, shard is not None)
+        scatter.start()
+        if shard is not None:
+            weight = Exchange(place, given[1], made[1], *rest)
+            weight.start()
+        scatter.run()
+        scatter.finish()
+        if shard is not None:
+            weight.spread()
+            weight.relay()
+            weight.finish()
+
+    return comm_call(body, number, outs, ins, scratch, args)
 
 
 def weights_out(grads, ranks, planes):
@@ -351,15 +833,16 @@
     hidden = tokens.reshape(-1, width).astype(jnp.float32)
     normed_one, factor_one = normalize(hidden)
     attn_in = (normed_one * gains[0]).astype(jnp.bfloat16)
-    seq_in = lax.all_gather(attn_in, "cp", axis=0, tiled=True)
     pairs = jnp.stack(
         [w_key.reshape(rows, KV_HEADS, HEAD), w_value.reshape(rows, KV_HEADS, HEAD)], axis=2
     ).reshape(rows, ranks, HEAD)
-    attn_w = weights_in(
-        jnp.concatenate(
-            [w_query.reshape(rows, ranks, HEAD), pairs, w_out.reshape(rows, ranks, HEAD)], axis=-1
-        )
-    )
+    attn_shard = jnp.concatenate(
+        [w_query.reshape(rows, ranks, HEAD), pairs, w_out.reshape(rows, ranks, HEAD)], axis=-1
+    ).reshape(rows, -1)
+    seq_in, attn_w, gate_part = front(ranks, planes, attn_in, attn_shard, w_gate)
+    seq_in = seq_in.reshape(-1, width)
+    attn_w = attn_w.reshape(width, -1)
+    gate_part = gate_part.reshape(width, -1)
     w_lin = attn_w[:, : 2 * HEAD]
     w_back = attn_w[:, 2 * HEAD :]
     lin = jnp.dot(seq_in, w_lin, preferred_element_type=jnp.float32)
@@ -382,17 +865,15 @@
     share_attn = lax.dot_general(
         attended_low, w_back, CONTRACT_LAST, preferred_element_type=jnp.float32
     )
-    attn_out = lax.psum_scatter(
-        share_attn.astype(jnp.bfloat16), "cp", scatter_dimension=0, tiled=True
-    ).astype(jnp.float32)
+    attn_out, up_part = column_scatter(1, ranks, planes, share_attn.astype(jnp.bfloat16), w_up)
+    up_part = up_part.reshape(width, -1)
     normed_two, factor_two = normalize(attn_out)
     middle_sum = hidden + normed_two * gains[1]
     normed_three, factor_three = normalize(middle_sum)
     ffn_in = (normed_three * gains[2]).astype(jnp.bfloat16)
-    gate_part, up_part, down_part = (
-        weights_in(piece.reshape(rows, ranks, -1)) for piece in (w_gate, w_up, w_down)
-    )
-    group_in = lax.all_gather(ffn_in, "cp", axis=0, tiled=True)
+    group_in, down_part = column_gather(2, ranks, planes, ffn_in, w_down)
+    group_in = group_in.reshape(-1, width)
+    down_part = down_part.reshape(width, -1)
     gate = jnp.dot(group_in, gate_part, preferred_element_type=jnp.float32)
     upper = jnp.dot(group_in, up_part, preferred_element_type=jnp.float32)
     activated = jax.nn.gelu(gate, approximate=True)
@@ -400,16 +881,15 @@
     share_out = lax.dot_general(
         inner_low, down_part, CONTRACT_LAST, preferred_element_type=jnp.float32
     )
-    ffn_out = lax.psum_scatter(
-        share_out.astype(jnp.bfloat16), "cp", scatter_dimension=0, tiled=True
-    ).astype(jnp.float32)
+    (ffn_out,) = column_scatter(3, ranks, planes, share_out.astype(jnp.bfloat16))
     normed_four, factor_four = normalize(ffn_out)
     result = middle_sum + normed_four * gains[3]
     output = result.astype(jnp.bfloat16).reshape(tokens.shape)
     grad_result = cotangent.reshape(-1, width).astype(jnp.float32)
     gain_four = jnp.sum(grad_result * normed_four, axis=0)
     grad_ffn_low = norm_back(grad_result * gains[3], normed_four, factor_four).astype(jnp.bfloat16)
-    group_grad = lax.all_gather(grad_ffn_low, "cp", axis=0, tiled=True)
+    (group_grad,) = column_gather(4, ranks, planes, grad_ffn_low)
+    group_grad = group_grad.reshape(-1, width)
     grad_inner = jnp.dot(group_grad, down_part, preferred_element_type=jnp.float32)
     unused_value, gelu_back = jax.vjp(partial(jax.nn.gelu, approximate=True), gate)
     grad_gate_low = gelu_back(grad_inner * upper)[0].astype(jnp.bfloat16)
@@ -417,9 +897,7 @@
     share_in = lax.dot_general(
         grad_gate_low, gate_part, CONTRACT_LAST, preferred_element_type=jnp.float32
     ) + lax.dot_general(grad_upper_low, up_part, CONTRACT_LAST, preferred_element_type=jnp.float32)
-    grad_ffn_in = lax.psum_scatter(
-        share_in.astype(jnp.bfloat16), "cp", scatter_dimension=0, tiled=True
-    ).astype(jnp.float32)
+    (grad_ffn_in,) = column_scatter(5, ranks, planes, share_in.astype(jnp.bfloat16))
     grad_gate, grad_up, grad_down = (
         weights_out(
             lax.dot_general(left, right, CONTRACT_FIRST, preferred_element_type=jnp.float32),
@@ -438,7 +916,8 @@
     grad_middle = grad_result + norm_back(grad_ffn_in * gains[2], normed_three, factor_three)
     gain_two = jnp.sum(grad_middle * normed_two, axis=0)
     grad_attn_low = norm_back(grad_middle * gains[1], normed_two, factor_two).astype(jnp.bfloat16)
-    seq_grad = lax.all_gather(grad_attn_low, "cp", axis=0, tiled=True)
+    (seq_grad,) = column_gather(6, ranks, planes, grad_attn_low)
+    seq_grad = seq_grad.reshape(-1, width)
     grad_att_low = jnp.dot(seq_grad, w_back, preferred_element_type=jnp.float32).astype(
         jnp.bfloat16
     )
@@ -468,9 +947,7 @@
     share_back = lax.dot_general(
         grad_lin, w_lin, CONTRACT_LAST, preferred_element_type=jnp.float32
     )
-    grad_attn_in = lax.psum_scatter(
-        share_back.astype(jnp.bfloat16), "cp", scatter_dimension=0, tiled=True
-    ).astype(jnp.float32)
+    (grad_attn_in,) = column_scatter(7, ranks, planes, share_back.astype(jnp.bfloat16))
     attn_sums = weights_out(
         jnp.concatenate(
             [

time: 1170 us -> 1050 us (0.90)
  Pallas kernels: 0 us -> 595 us
  waiting for transfers between devices: 705 us -> 112 us
  blocking collectives: 202 us -> 75.6 us
  matrix products: 120 us -> 132 us
    pallas_call x0 -> x8, Pallas kernels: none -> 595 us  [comm_call(): pl.pallas_call(body, out_shape=[shape for shape, spec in outs], in_specs=...]
    all_gather x8 -> x0, waiting for transfers between devices: 346 us -> none  [the longest x4 187 us: weights_in(): lax.all_gather(pieces.reshape(-1, columns), 'fsdp', axis=0, tiled=True)]
    all_to_all x4 -> x1, blocking collectives: 166 us -> 26.9 us  [weights_out(): lax.all_to_all(sums.reshape(ranks, rows, -1), 'cp', split_axis=0, concat_...]
    reduce_scatter x4 -> x0, waiting for transfers between devices: 136 us -> none  [the longest x1 53.5 us: by_heads(): lax.psum_scatter(share_in.astype(jnp.bfloat16), 'cp', scatter_dimension=0...]
    reduce_scatter x4, waiting for transfers between devices: 167 us -> 110 us  [weights_out(): sums = lax.psum_scatter(parted, 'fsdp', scatter_dimension=0, tiled=True)]
    all_to_all x4 -> x3, waiting for transfers between devices: 53.2 us -> 0.01 us  [weights_out(): lax.all_to_all(sums.reshape(ranks, rows, -1), 'cp', split_axis=0, concat_...]
    reshape x4 -> x0, local copies, waits for them, and re-layouts: 20 us -> none  [weights_in(): whole = whole.reshape(-1, ranks, rows, columns).transpose(1, 0, 2, 3)]
    dot_general x0 -> x2, local copies, waits for them, and re-layouts: none -> 13.4 us  [the longest x1 6.71 us: by_heads(): lax.dot_general(seq_grad, attended_low, CONTRACT_FIRST, preferred_element...]
  transfers between devices with their start and end apart: 22 -> 9, of which waited for: 18 -> 4; matrix products, arithmetic and copies ran while one was open for 9% -> 7% of each run, Pallas kernels for 0% -> 6%
where the time goes in v2:
time: 1050 us; the launch traced here: 1030 us
  Pallas kernels  595 us (57%)
  matrix products  132 us (13%)
  waiting for transfers between devices  112 us (11%)
  blocking collectives  75.6 us (7%)
  local copies, waits for them, and re-layouts  42.1 us (4%)
  other arithmetic  39.5 us (4%)
  starting transfers between devices  23.3 us (2%)
  between operations  15.3 us (1%)
    pallas_call x8, Pallas kernels, comm_call(): pl.pallas_call(body, out_shape=[shape for shape, spec in outs], in_specs=...  595 us
    reduce_scatter x4, waiting for transfers between devices, weights_out(): sums = lax.psum_scatter(parted, 'fsdp', scatter_dimension=0, tiled=True)  110 us
    unnamed x1, blocking collectives  48.7 us
    dot_general x3, matrix products, by_heads(): lax.dot_general(left, right, CONTRACT_FIRST, preferred_element_type=jnp.f...  27.4 us
    all_to_all x1, blocking collectives, weights_out(): lax.all_to_all(sums.reshape(ranks, rows, -1), 'cp', split_axis=0, concat_...  26.9 us
  transfers between devices with their start and end apart: 9, of which 4 were waited for; matrix products, arithmetic and copies ran while one was open for 7% of the time, Pallas kernels for 6%

profile of v2, /device:TPU:9, one launch (start us, length us, event | category | flops | bytes accessed | tf_op | source)
XLA Modules:
  0.0 1034.2 jit_solution(13046656302140716117)
XLA Ops:
  18.0 134.9 %shard_map.186 = (bf16[8,128,2304]{2,1,0:T(8,128)(2,1)}, bf16[8,4,72,768]{3,2,1,0:T(8,128)(2,1)}, bf16[8,4,72,1152]{3,2,1,0:T(8,128)(2,1)}) custom-call(bf16[128,2304]{1,0:T(8,128)(2,1)} %fusion.22.x, bf16[72,6144]{1,0:T(8,128)(2,1)} %bitcast.211, bf16[72,9216]{1,0:T(8,128)(2,1)} %wg.1), custom_call_target="tpu_custom_call" | custom-call | tf_op jit(solution)/shard_map/pallas_call | solution.py:670
  153.0 5.3 fusion.10
  158.3 2.5 fusion.68
  160.8 3.5 collective-permute-start
  171.1 5.1 convolution_convert_fusion.5
  176.2 121.1 %shard_map.187 = (f32[128,2304]{1,0:T(8,128)}, bf16[8,4,72,1152]{3,2,1,0:T(8,128)(2,1)}) custom-call(bf16[8,128,2304]{2,1,0:T(8,128)(2,1)} %bitcast.190, bf16[72,9216]{1,0:T(8,128)(2,1)} %refs_1_.2), custom_call_target="tpu_custom_call" | custom-call | tf_op jit(solution)/shard_map/pallas_call | solution.py:670
  302.1 91.4 %shard_map.188 = (bf16[8,128,2304]{2,1,0:T(8,128)(2,1)}, bf16[8,4,72,1152]{3,2,1,0:T(8,128)(2,1)}) custom-call(bf16[128,2304]{1,0:T(8,128)(2,1)} %multiply_convert_fusion.4.refs_0_, bf16[72,9216]{1,0:T(8,128)(2,1)} %refs_1_.3), custom_call_target="tpu_custom_call" | custom-call | tf_op jit(solution)/shard_map/pallas_call | solution.py:670
  393.5 9.8 fusion.85
  403.4 12.5 %multiply_convert_fusion.1 = (bf16[1024,1152]{1,0:T(8,128)(2,1)S(1)}, f32[1024,1152]{1,0:T(8,128)}) fusion(f32[1024,1152]{1,0:T(8,128)S(1)} %fusion.85, bf16[1024,2304]{1,0:T(8,128)(2,1)S(1)} %bitcast.248, bf16[2304,1152]{1,0:T(8,128)(2,1)} %bitcast.239), kind=kOutput, calls=%fused_computation.17 | convolution fusion | flops 5447614464 | bytes 21823488 | tf_op jit(solution)/shard_map/dot_general | solution.py:878
  416.0 7.9 convolution_convert_fusion.4
  423.9 49.7 %shard_map.189 = f32[128,2304]{1,0:T(8,128)} custom-call(bf16[8,128,2304]{2,1,0:T(8,128)(2,1)} %bitcast.208), custom_call_target="tpu_custom_call" | custom-call | tf_op jit(solution)/shard_map/pallas_call | solution.py:670
  475.0 2.3 fusion.17
  477.3 2.7 fusion.16
  480.0 42.5 %shard_map.190 = bf16[8,128,2304]{2,1,0:T(8,128)(2,1)} custom-call(bf16[128,2304]{1,0:T(8,128)(2,1)} %get-tuple-element.48.refs_0_), custom_call_target="tpu_custom_call" | custom-call | tf_op jit(solution)/shard_map/pallas_call | solution.py:670
  522.5 14.3 %multiply_convert_fusion = (bf16[1024,1152]{1,0:T(8,128)(2,1)S(1)}, bf16[1024,1152]{1,0:T(8,128)(2,1)S(1)}) fusion(f32[1024,1152]{1,0:T(8,128)} %copy-done.45, f32[1024,1152]{1,0:T(8,128)} %get-tuple-element.61, bf16[1024,2304]{1,0:T(8,128)(2,1)} %bitcast.209, bf16[2304,1152]{1,0:T(8,128)(2,1)} %bitcast.241), kind=kOutput, calls=%fused_computation.16 | convolution fusion | flops 5464129536 | bytes 24182784 | tf_op jit(solution)/shard_map/dot_general | solution.py:893
  536.8 10.5 %fusion.86 = f32[1024,2304]{1,0:T(8,128)S(1)} fusion(bf16[1024,1152]{1,0:T(8,128)(2,1)S(1)} %get-tuple-element.40, bf16[2304,1152]{1,0:T(8,128)(2,1)} %bitcast.238), kind=kOutput, calls=%fused_computation.158 | convolution fusion | flops 5435817984 | bytes 17104896 | tf_op jit(solution)/shard_map/dot_general | solution.py:897
  547.4 10.6 %add_convert_fusion = bf16[1024,2304]{1,0:T(8,128)(2,1)} fusion(f32[1024,2304]{1,0:T(8,128)S(1)} %fusion.86, bf16[1024,1152]{1,0:T(8,128)(2,1)S(1)} %get-tuple-element.39, bf16[2304,1152]{1,0:T(8,128)(2,1)} %bitcast.240), kind=kOutput, calls=%fused_computation.3 | convolution fusion | flops 5440536576 | bytes 21823488 | tf_op jit(solution)/shard_map/dot_general | solution.py:899
  558.0 53.9 %shard_map.191 = f32[128,2304]{1,0:T(8,128)} custom-call(bf16[8,128,2304]{2,1,0:T(8,128)(2,1)} %bitcast.207), custom_call_target="tpu_custom_call" | custom-call | tf_op jit(solution)/shard_map/pallas_call | solution.py:670
  611.9 2.3 multiply_reduce_fusion.1
  614.2 2.9 multiply_reduce_fusion.2
  619.3 42.5 %shard_map.192 = bf16[8,128,2304]{2,1,0:T(8,128)(2,1)} custom-call(bf16[128,2304]{1,0:T(8,128)(2,1)} %multiply_convert_fusion.3.refs_0_), custom_call_target="tpu_custom_call" | custom-call | tf_op jit(solution)/shard_map/pallas_call | solution.py:670
  661.9 4.2 convolution_convert_fusion.8
  668.0 2.5 multiply_convert_fusion.2
  671.3 3.4 broadcast_select_fusion
  674.7 2.2 collective-permute-start.1
  677.0 6.7 copy.53
  683.6 6.7 copy.55
  692.2 3.9 convolution_convert_fusion.7
  697.7 2.5 fusion.60
  700.2 3.7 convolution_convert_fusion.6
  704.2 2.0 copy.56
  706.3 9.2 convolution_convert_fusion
  715.5 2.8 copy.68
  718.4 9.2 convolution_convert_fusion.1
  727.6 2.8 copy.65
  730.4 9.0 convolution_convert_fusion.2
  739.5 2.8 copy.62
  742.3 12.6 %reduce-scatter.6.cloned.1.call-done = bf16[576,768]{1,0:T(8,128)(2,1)} async-done(((bf16[2304,768]{1,0:T(8,128)(2,1)}), bf16[576,768]{1,0:T(8,128)(2,1)}) %reduce-scatter.6.cloned.1.call-update) | async-done | bytes 884752 | tf_op jit(solution)/shard_map/reduce_scatter | solution.py:797
  754.9 26.9 %all_to_all.16 = bf16[8,72,1,768]{3,1,2,0:T(8,128)(2,1)} all-to-all(bf16[8,72,1,768]{3,1,2,0:T(8,128)(2,1)} %bitcast.225), channel_id=1, replica_groups=mesh['cp'=8,'fsdp'=4] {'cp'}, dimensions={0} | all-to-all | bytes 1769472 | tf_op jit(solution)/shard_map/all_to_all | solution.py:798
  781.8 38.0 %reduce-scatter.12.cloned.1.call-done = bf16[576,1152]{1,0:T(8,128)(2,1)} async-done(((bf16[2304,1152]{1,0:T(8,128)(2,1)}), bf16[576,1152]{1,0:T(8,128)(2,1)}) %reduce-scatter.12.cloned.1.call-update) | async-done | bytes 1327120 | tf_op jit(solution)/shard_map/reduce_scatter | solution.py:797
  819.8 5.6 all-to-all-start.3
  825.4 59.3 %reduce-scatter.10.cloned.1.call-done = bf16[576,1152]{1,0:T(8,128)(2,1)} async-done(((bf16[2304,1152]{1,0:T(8,128)(2,1)}), bf16[576,1152]{1,0:T(8,128)(2,1)}) %reduce-scatter.10.cloned.1.call-update) | async-done | bytes 1327120 | tf_op jit(solution)/shard_map/reduce_scatter | solution.py:797
  884.7 5.9 all-to-all-start.2
  890.7 6.1 convolution_convert_fusion.3
  896.8 58.6 %shard_map.193 = f32[128,2304]{1,0:T(8,128)} custom-call(bf16[8,128,2304]{2,1,0:T(8,128)(2,1)} %bitcast.206), custom_call_target="tpu_custom_call" | custom-call | tf_op jit(solution)/shard_map/pallas_call | solution.py:670
  957.2 2.7 fusion.26
  959.9 5.9 all-to-all-start.1
  965.8 48.7 %all-reduce = f32[2304,4]{0,1:T(4,128)S(1)} all-reduce(f32[2304,4]{0,1:T(4,128)S(1)} %pad_maximum_fusion.9), channel_id=2, replica_groups=mesh['cp'=8,'fsdp'=4] {'cp','fsdp'}, use_global_device_ids=true, to_apply=%region_15.16.clone | all-reduce | flops 9216 | bytes 73728
  (184 shorter events, 46.8 us)
Async XLA Ops:
  7.2 9.8 copy-start.3
  7.2 747.7 %reduce-scatter.6.cloned.1.call-start = ((), (), s32[]{:S(2)}) async-start(), calls=%async_computation.8 | async-start | bytes 4423680 | tf_op jit(solution)/shard_map/reduce_scatter | solution.py:797
  7.3 151.0 %copy-start.40 = (f32[128]{0:T(128)}, f32[128]{0:T(128)S(1)}, u32[]{:S(2)}) copy-start(f32[128]{0:T(128)S(1)} %multiply_exponential_fusion) | copy-start | bytes 1540
  9.4 8.7 copy-start.36
  9.5 159.3 %copy-start.24 = (s32[1024]{0:T(1024)}, s32[1024]{0:T(1024)S(1)}, u32[]{:S(2)}) copy-start(s32[1024]{0:T(1024)S(1)} %add.117) | copy-start | bytes 12292
  9.5 148.7 %copy-start.29 = (f32[1024]{0:T(1024)}, f32[1024]{0:T(1024)S(1)}, u32[]{:S(2)}) copy-start(f32[1024]{0:T(1024)S(1)} %convert_element_type.140) | copy-start | bytes 12292
  11.2 5.9 copy-start.21
  160.7 6.3 copy-start.17
  160.7 6.3 copy-start.19
  160.8 8.1 copy-start.15
  160.8 5.1 collective-permute-start
  171.1 5.1 copy-start.10
  300.4 102.9 %copy-start.35 = (f32[128]{0:T(128)}, f32[128]{0:T(128)S(1)}, u32[]{:S(2)}) copy-start(f32[128]{0:T(128)S(1)} %add_rsqrt_fusion.2) | copy-start | bytes 1540
  393.5 9.9 copy-start.42
  393.5 22.4 %slice-start.2 = ((s8[5308416]{0:T(1024)(128)(4,1)}), s8[4194304]{0:T(1024)(128)(4,1)S(1)}, s32[]{:S(2)}) async-start(s8[5308416]{0:T(1024)(128)(4,1)} %bitcast.242), calls=%async_computation.14 | async-start | bytes 8388608
  403.4 12.6 %copy-start.45 = (f32[1024,1152]{1,0:T(8,128)}, f32[1024,1152]{1,0:T(8,128)S(1)}, u32[]{:S(2)}) copy-start(f32[1024,1152]{1,0:T(8,128)S(1)} %fusion.85) | copy-start | bytes 14155780
  403.4 12.6 %slice-start.3 = ((s8[5308416]{0:T(1024)(128)(4,1)}), s8[1114112]{0:T(1024)(128)(4,1)S(1)}, s32[]{:S(2)}) async-start(s8[5308416]{0:T(1024)(128)(4,1)} %bitcast.242), calls=%async_computation.15 | async-start | bytes 2228224
  415.9 8.0 copy-start.48
  423.9 51.1 %copy-start.7 = (bf16[1,2,64,2304]{3,2,1,0:T(8,128)(2,1)S(1)}, bf16[1,2,64,2304]{3,2,1,0:T(8,128)(2,1)}, u32[]{:S(2)}) copy-start(bf16[1,2,64,2304]{3,2,1,0:T(8,128)(2,1)} %param.21) | copy-start | bytes 1769476
  536.8 10.5 %copy-start.47 = (bf16[1024,1152]{1,0:T(8,128)(2,1)}, bf16[1024,1152]{1,0:T(8,128)(2,1)S(1)}, u32[]{:S(2)}) copy-start(bf16[1024,1152]{1,0:T(8,128)(2,1)S(1)} %get-tuple-element.40) | copy-start | bytes 7077892
  536.8 10.5 %copy-start.46 = (bf16[1024,1152]{1,0:T(8,128)(2,1)}, bf16[1024,1152]{1,0:T(8,128)(2,1)S(1)}, u32[]{:S(2)}) copy-start(bf16[1024,1152]{1,0:T(8,128)(2,1)S(1)} %get-tuple-element.39) | copy-start | bytes 7077892
  611.9 6.3 copy-start
  611.9 6.3 copy-start.23
  611.9 6.3 copy-start.39
  661.8 4.3 copy-start.2
  661.8 4.3 copy-start.16
  661.8 4.3 copy-start.25
  661.8 4.3 copy-start.32
  661.8 4.3 copy-start.34
  674.7 21.4 %collective-permute-start.1 = (f32[1024,256]{0,1:T(8,128)}, f32[1024,256]{0,1:T(8,128)}, u32[]{:S(2)}, u32[]{:S(2)}) collective-permute-start(f32[1024,256]{0,1:T(8,128)} %get-tuple-element.64), channel_id=1, source_target_pairs={{0,4},{4,0},{8,12},{12,8},{16,20},{20,16},{24,28},{28,24},{1,5},{5... | collective-permute-start | bytes 3145736 | tf_op jit(solution)/shard_map/ppermute | solution.py:937
  692.2 8.0 slice-start
  692.2 5.5 copy-start.30
  692.2 5.5 copy-start.41
  692.2 8.0 slice-start.1
  706.2 113.6 %reduce-scatter.12.cloned.1.call-start = ((), (), s32[]{:S(2)}) async-start(), calls=%async_computation.11 | async-start | bytes 6635520 | tf_op jit(solution)/shard_map/reduce_scatter | solution.py:797
  718.3 166.4 %reduce-scatter.10.cloned.1.call-start = ((), (), s32[]{:S(2)}) async-start(), calls=%async_computation.10 | async-start | bytes 6635520 | tf_op jit(solution)/shard_map/reduce_scatter | solution.py:797
  730.4 229.5 %reduce-scatter.8.cloned.1.call-start = ((), (), s32[]{:S(2)}) async-start(), calls=%async_computation.9 | async-start | bytes 6635520 | tf_op jit(solution)/shard_map/reduce_scatter | solution.py:797
  742.3 148.3 %copy-start.26 = (f32[2304]{0:T(1024)S(1)}, f32[2304]{0:T(1024)}, u32[]{:S(2)}) copy-start(f32[2304]{0:T(1024)} %get-tuple-element.30) | copy-start | bytes 27652
  742.3 148.4 %copy-start.27 = (f32[2304]{0:T(1024)S(1)}, f32[2304]{0:T(1024)}, u32[]{:S(2)}) copy-start(f32[2304]{0:T(1024)} %get-tuple-element.26) | copy-start | bytes 27652
  742.3 148.4 %copy-start.28 = (f32[2304]{0:T(1024)S(1)}, f32[2304]{0:T(1024)}, u32[]{:S(2)}) copy-start(f32[2304]{0:T(1024)} %get-tuple-element.24) | copy-start | bytes 27652
  819.8 64.9 %all-to-all-start.3 = ((bf16[8,72,1,1152]{3,1,2,0:T(8,128)(2,1)}), bf16[8,72,1,1152]{3,1,2,0:T(8,128)(2,1)S(1)}, u32[]{:S(2)}, u32[]{:S(2)}) async-start(bf16[8,72,1,1152]{3,1,2,0:T(8,128)(2,1)} %bitcast.219), calls=%async_computation.7 | async-start | bytes 2654208 | tf_op jit(solution)/shard_map/all_to_all | solution.py:798
  884.7 12.0 %copy-start.8 = (bf16[8,72,1,1152]{3,1,2,0:T(8,128)(2,1)}, bf16[8,72,1,1152]{3,1,2,0:T(8,128)(2,1)S(1)}, u32[]{:S(2)}) copy-start(bf16[8,72,1,1152]{3,1,2,0:T(8,128)(2,1)S(1)} %all-to-all-done.3) | copy-start | bytes 3981316
  884.7 75.1 %all-to-all-start.2 = ((bf16[8,72,1,1152]{3,1,2,0:T(8,128)(2,1)}), bf16[8,72,1,1152]{3,1,2,0:T(8,128)(2,1)}, u32[]{:S(2)}, u32[]{:S(2)}) async-start(bf16[8,72,1,1152]{3,1,2,0:T(8,128)(2,1)} %bitcast.218), calls=%async_computation.5 | async-start | bytes 2654208 | tf_op jit(solution)/shard_map/all_to_all | solution.py:798
  896.8 58.6 %copy-start.4 = (bf16[1,2,64,2304]{3,2,1,0:T(8,128)(2,1)S(1)}, bf16[1,2,64,2304]{3,2,1,0:T(8,128)(2,1)}, u32[]{:S(2)}) copy-start(bf16[1,2,64,2304]{3,2,1,0:T(8,128)(2,1)} %param.11) | copy-start | bytes 1769476
  896.8 58.6 %copy-start.22 = (f32[2304]{0:T(1024)S(1)}, f32[2304]{0:T(1024)}, u32[]{:S(2)}) copy-start(f32[2304]{0:T(1024)} %copy-done.21) | copy-start | bytes 27652
  896.8 58.7 %copy-start.37 = (f32[128]{0:T(128)S(1)}, f32[128]{0:T(128)}, u32[]{:S(2)}) copy-start(f32[128]{0:T(128)} %copy-done.36) | copy-start | bytes 1540
  896.8 60.4 %copy-start.6 = (f32[128,2304]{1,0:T(8,128)S(1)}, f32[128,2304]{1,0:T(8,128)}, u32[]{:S(2)}) copy-start(f32[128,2304]{1,0:T(8,128)} %copy-done.5) | copy-start | bytes 3538948
  959.9 65.5 %all-to-all-start.1 = ((bf16[8,72,1,1152]{3,1,2,0:T(8,128)(2,1)}), bf16[8,72,1,1152]{3,1,2,0:T(8,128)(2,1)S(1)}, u32[]{:S(2)}, u32[]{:S(2)}) async-start(bf16[8,72,1,1152]{3,1,2,0:T(8,128)(2,1)} %bitcast.217), calls=%async_computation.3 | async-start | bytes 2654208 | tf_op jit(solution)/shard_map/all_to_all | solution.py:798
  (14 other events, 39.9 us)
Sparse Core Ops, SparseCore 0:
  706.4 48.4 reduce-scatter.5
  757.9 61.8 reduce-scatter.11
  822.8 61.8 reduce-scatter.9
  887.6 61.8 reduce-scatter.7
